TPU v7x, 1024 devices: a whole 8x8x8 slice. The times are simulated.
1024 devices in a mesh: comp: 2 (over core), blk: 512 (over y, z, x).
Axes of the slice: x: 8, y: 8, z: 8, core: 2. Of those that a mesh axis runs over, the one named last changes fastest.
Arguments:
- initial: float32 [2, 5, 4096, 2048], P('comp', None, 'blk'), may hold values from -3 to 3
- ice_forcing: float32 [5, 4096, 2048], P(None, 'blk'), may hold values from -2 to 4, as said below
- ocean_current: float32 [2, 4096, 2048], P(None, 'blk'), may hold values from -1 to 1
- ice_cover: int32 [4096, 2048], P('blk'), may hold values from 0 to 1, as said below
- targets: int32 [2, 4096, 2048], P(None, 'blk'), may hold values from 0 to 32767, as said below
- weights: int32 [2, 4096, 2048], P(None, 'blk'), may hold values from 1 to 4
Outputs:
- state_out: float32 [2, 5, 4096, 2048], P('comp', None, 'blk')
- coupled: float32 [2, 3, 4096, 2048], P('comp', None, 'blk')
Inputs may be any that keep to these rules, and one draw needn't show every extreme that they name: `ice_forcing`: channel 0 (mass) lies in 0.5 to 4, channel 1 (strength) and channel 4 (melt rate) in 0.2 to 2, channels 2 and 3 (wind stress) in -2 to 2. `ice_cover`: the share of ice-covered cells differs from strip to strip of 8 rows. `targets`: an entry of an ice cell at row r of its strip names an ocean row of the window no earlier than r.
All inputs are finite; a program needn't handle non-finite values.
Results may differ from a plain program's by a relative error of at most 0.0003.
Values sent between devices are 32-bit elements; how exact they have to be, the bound alone decides.
No kernel may reach another device: no remote copies, remote signals or barrier semaphores. Data moves between devices by JAX's collectives and lax.ppermute only.
A program may use at most 128 MiB of HBM per device.

v0:
```python
import jax
import jax.numpy as jnp
from jax import lax
from jax.sharding import PartitionSpec as P

SUBCYCLES = 16


relax_rate = 0.5
ecc_sq = 4.0
delta_floor = 0.1
coriolis = 0.1
drag_coef = 1.0
inertia = 4.0
courant = 0.2
dilution = 0.5
weight_norm = 4.0
level_speed = (1.0, 0.8, 0.6, 0.45, 0.3)


def extended_2(block, sides, width):
    for axis, dim in sides:
        count = lax.axis_size(axis)
        forward = [(i, i + 1) for i in range(count - 1)]
        backward = [(target, source) for source, target in forward]
        low = lax.ppermute(
            lax.slice_in_dim(block, block.shape[dim] - width, None, axis=dim), axis, forward
        )
        high = lax.ppermute(lax.slice_in_dim(block, 0, width, axis=dim), axis, backward)
        block = jnp.concatenate([low, block, high], axis=dim)
    return block


def shifted(value, axis, steps):
    count = lax.axis_size(axis)
    first, last = (max(0, -steps), min(count, count - steps))
    return lax.ppermute(value, axis, [(source, source + steps) for source in range(first, last)])


def from_behind(value, axis, steps):
    count = lax.axis_size(axis)
    pairs = [(source, (source + steps) % count) for source in range(count)]
    return lax.ppermute(value, axis, pairs)


def along_rows(field):
    return 0.5 * (field[..., 2:, :] - field[..., :-2, :])


def across(field):
    padded = jnp.pad(field, [(0, 0)] * (field.ndim - 1) + [(1, 1)])
    return 0.5 * (padded[..., 2:] - padded[..., :-2])


def ice_step(fields, forcing, current, covered):
    vel_x = fields[0]
    vel_y = fields[1]
    strain_d = along_rows(vel_x) + across(vel_y[1:-1])
    strain_t = along_rows(vel_x) - across(vel_y[1:-1])
    strain_s = across(vel_x[1:-1]) + along_rows(vel_y)
    delta = jnp.sqrt(
        strain_d * strain_d
        + (strain_t * strain_t + strain_s * strain_s) / ecc_sq
        + delta_floor * delta_floor
    )
    press = forcing[1, 1:-1] * covered[1:-1]
    sig_one = (fields[2, 1:-1] + relax_rate * press * (strain_d / delta - 1.0)) / (1.0 + relax_rate)
    sig_two = (fields[3, 1:-1] + relax_rate * press * strain_t / (ecc_sq * delta)) / (
        1.0 + relax_rate
    )
    sig_shear = (fields[4, 1:-1] + relax_rate * press * strain_s / (2.0 * ecc_sq * delta)) / (
        1.0 + relax_rate
    )
    sig_xx = 0.5 * (sig_one + sig_two)
    sig_yy = 0.5 * (sig_one - sig_two)
    force_x = along_rows(sig_xx) + across(sig_shear[1:-1])
    force_y = along_rows(sig_shear) + across(sig_yy[1:-1])
    beta = inertia * forcing[0, 2:-2]
    old_x = vel_x[2:-2]
    old_y = vel_y[2:-2]
    denom = beta + drag_coef
    new_x = (
        covered[2:-2]
        * (
            beta * old_x
            + coriolis * beta * old_y
            + force_x
            + forcing[2, 2:-2]
            + drag_coef * current[0, 2:-2]
        )
        / denom
    )
    new_y = (
        covered[2:-2]
        * (
            beta * old_y
            - coriolis * beta * old_x
            + force_y
            + forcing[3, 2:-2]
            + drag_coef * current[1, 2:-2]
        )
        / denom
    )
    return jnp.stack([new_x, new_y, sig_one[1:-1], sig_two[1:-1], sig_shear[1:-1]])


def ocean_step(tracer, current):
    speed = jnp.asarray(level_speed, jnp.float32)[:, None, None]
    centre = tracer[:, 2:-2]
    below = centre - tracer[:, 1:-3]
    above = tracer[:, 3:-1] - centre
    padded = jnp.pad(centre, ((0, 0), (0, 0), (1, 1)))
    left_diff = centre - padded[:, :, :-2]
    right_diff = padded[:, :, 2:] - centre
    speed_x = speed * current[0, 2:-2][None]
    speed_y = speed * current[1, 2:-2][None]
    change = (
        jnp.maximum(speed_x, 0.0) * below
        + jnp.minimum(speed_x, 0.0) * above
        + jnp.maximum(speed_y, 0.0) * left_diff
        + jnp.minimum(speed_y, 0.0) * right_diff
    )
    return centre - courant * change


def coupling_terms(fields, forcing, current, covered):
    stress_x = covered * drag_coef * (fields[0] - current[0])
    stress_y = covered * drag_coef * (fields[1] - current[1])
    fresh = forcing[4] * covered * jnp.sqrt(1.0 + fields[0] * fields[0] + fields[1] * fields[1])
    return jnp.stack([stress_x, stress_y, fresh])


def remap_window(values, targets, weights):
    scaled = weights.astype(jnp.float32) / weight_norm
    window_size = 2 * values.shape[1] * values.shape[2]
    flat_targets = targets.reshape(-1)

    def spread(single):
        return jax.ops.segment_sum(
            (single[None] * scaled).reshape(-1), flat_targets, num_segments=window_size
        )

    return jax.vmap(spread)(values)


def body(initial, ice_forcing, ocean_current, ice_cover, targets, weights):
    depth = 2
    width = 2 * depth
    is_ice = lax.axis_index("comp") == 0
    row_count = initial.shape[2]
    col_count = initial.shape[3]
    covered = ice_cover.astype(jnp.float32)
    statics = jnp.concatenate([ice_forcing, ocean_current, covered[None]], axis=0)
    static_ext = extended_2(statics, (("blk", 1),), width)
    forcing_ext = static_ext[:5]
    current_ext = static_ext[5:7]
    cover_ext = static_ext[7]
    empty_total = jnp.zeros((3, row_count, col_count), jnp.float32)

    def ice_turns(extended):
        fields = extended
        total = empty_total
        for turn in range(depth):
            lower = 2 * turn
            upper = row_count + 2 * width - 2 * turn
            fields = ice_step(
                fields,
                forcing_ext[:, lower:upper],
                current_ext[:, lower:upper],
                cover_ext[lower:upper],
            )
            own_start = width - 2 * (turn + 1)
            own_fields = fields[:, own_start : own_start + row_count]
            total = total + coupling_terms(own_fields, ice_forcing, ocean_current, covered)
        return (fields, total)

    def ocean_turns(extended):
        fields = extended
        for turn in range(depth):
            lower = 2 * turn
            upper = row_count + 2 * width - 2 * turn
            fields = ocean_step(fields, current_ext[:, lower:upper])
        return (fields, empty_total)

    def advance(step_index, carry):
        fields, total = carry
        extended = extended_2(fields, (("blk", 1),), width)
        fields, extra = lax.cond(is_ice, ice_turns, ocean_turns, extended)
        return (fields, total + extra)

    fields, total = lax.fori_loop(0, SUBCYCLES // depth, advance, (initial[0], empty_total))
    average = total / SUBCYCLES
    empty_window = jnp.zeros((3, 2 * row_count * col_count), jnp.float32)

    def window_sums(values):
        return remap_window(values, targets, weights)

    def no_window(values):
        return empty_window

    partial_sums = lax.cond(is_ice, window_sums, no_window, average)
    window = shifted(partial_sums, "comp", 1)
    half_size = row_count * col_count
    from_before = from_behind(window[:, half_size:], "blk", 1)
    flux = (window[:, :half_size] + from_before).reshape(3, row_count, col_count)

    def ice_result(fields, flux):
        return (fields, average)

    def ocean_result(fields, flux):
        salinity = jnp.concatenate([fields[:1] - dilution * flux[2][None], fields[1:]], axis=0)
        return (salinity, flux)

    final_state, coupled = lax.cond(is_ice, ice_result, ocean_result, fields, flux)
    return (final_state[None], coupled[None])


def solution(mesh):
    placed = (
        P("comp", None, "blk", None),
        P(None, "blk", None),
        P(None, "blk", None),
        P("blk", None),
        P(None, "blk", None),
        P(None, "blk", None),
    )
    return jax.shard_map(
        body,
        mesh=mesh,
        in_specs=placed,
        out_specs=(P("comp", None, "blk", None), P("comp", None, "blk", None)),
        check_vma=False,
    )
```

profile of v0, /device:TPU:65, one launch (start us, length us, event | category | flops | bytes accessed | tf_op | source)
XLA Modules:
  0.0 457.2 jit_solution(10752953261166834178)
XLA Ops:
  0.6 1.7 copy.50
  4.4 3.1 collective-permute-start.2
  7.5 17.9 %collective-permute-start.3 = (f32[8,4,2048]{2,1,0:T(4,128)S(1)}, f32[8,4,2048]{2,1,0:T(4,128)S(1)}, u32[]{:S(2)}, u32[]{:S(2)}) collective-permute-start(f32[8,4,2048]{2,1,0:T(4,128)S(1)} %get-tuple-element.306), channel_id=1, source_target_pairs={{1,0},{2,1},{3,2},{4,3},{5,4},{6,5},{7,6},{8,7},{9,8},{10,9},{11,1... | collective-permute-start | bytes 786440 | tf_op jit(solution)/shard_map/ppermute | solution.py:29
  25.5 4.0 collective-permute-done.2
  32.5 160.5 %while.15 = (s32[]{:T(128)}, f32[5,8,2048]{2,1,0:T(8,128)}, f32[3,8,2048]{2,1,0:T(8,128)S(1)}, pred[]{:T(512)}, f32[2,16,2048]{2,1,0:T(8,128)S(1)}, /*index=5*/f...) while((s32[]{:T(128)}, f32[5,8,2048]{2,1,0:T(8,128)}, ...), condition=%wide.region_3.4_spmd.clone.clone.clone, body=%wide.region_0.3_spmd.sunk.clone.clone.clone.sunk | while | flops 4530180 | bytes 15696172 | solution.py:191
  33.7 9.5 %collective-permute-start = (f32[5,4,2048]{2,1,0:T(4,128)S(1)}, f32[5,4,2048]{2,1,0:T(4,128)S(1)}, u32[]{:S(2)}, u32[]{:S(2)}) collective-permute-start(f32[5,4,2048]{2,1,0:T(4,128)S(1)} %get-tuple-element.374), channel_id=1, source_target_pairs={{1,0},{2,1},{3,2},{4,3},{5,4},{6,5},{7,6},{8,7},{9,8},{10,9},{11,1... | collective-permute-start | bytes 491528 | tf_op jit(solution)/shard_map/while/body/eval_jaxpr/ppermute | solution.py:29
  43.3 1.9 collective-permute-start.1
  45.5 9.3 %collective-permute-done.1 = f32[5,4,2048]{2,1,0:T(4,128)S(1)} collective-permute-done((f32[5,4,2048]{2,1,0:T(4,128)S(1)}, f32[5,4,2048]{2,1,0:T(4,128)S(1)}, u32[]{:S(2)}, u32[]{:S(2)}) %collective-permute-start.1) | collective-permute-done | bytes 163872 | tf_op jit(solution)/shard_map/while/body/eval_jaxpr/ppermute | solution.py:26
  55.8 3.1 conditional.10
  60.2 1.9 collective-permute-start
  62.1 3.4 collective-permute-start.1
  66.3 7.4 %collective-permute-done.1 = f32[5,4,2048]{2,1,0:T(4,128)S(1)} collective-permute-done((f32[5,4,2048]{2,1,0:T(4,128)S(1)}, f32[5,4,2048]{2,1,0:T(4,128)S(1)}, u32[]{:S(2)}, u32[]{:S(2)}) %collective-permute-start.1) | collective-permute-done | bytes 163872 | tf_op jit(solution)/shard_map/while/body/eval_jaxpr/ppermute | solution.py:26
  74.7 3.1 conditional.10
  76.1 1.7 fusion.85
  79.1 1.9 collective-permute-start
  81.0 3.4 collective-permute-start.1
  85.2 7.4 %collective-permute-done.1 = f32[5,4,2048]{2,1,0:T(4,128)S(1)} collective-permute-done((f32[5,4,2048]{2,1,0:T(4,128)S(1)}, f32[5,4,2048]{2,1,0:T(4,128)S(1)}, u32[]{:S(2)}, u32[]{:S(2)}) %collective-permute-start.1) | collective-permute-done | bytes 163872 | tf_op jit(solution)/shard_map/while/body/eval_jaxpr/ppermute | solution.py:26
  93.6 3.1 conditional.10
  98.0 1.9 collective-permute-start
  99.9 3.4 collective-permute-start.1
  104.3 7.1 %collective-permute-done.1 = f32[5,4,2048]{2,1,0:T(4,128)S(1)} collective-permute-done((f32[5,4,2048]{2,1,0:T(4,128)S(1)}, f32[5,4,2048]{2,1,0:T(4,128)S(1)}, u32[]{:S(2)}, u32[]{:S(2)}) %collective-permute-start.1) | collective-permute-done | bytes 163872 | tf_op jit(solution)/shard_map/while/body/eval_jaxpr/ppermute | solution.py:26
  112.5 3.1 conditional.10
  113.9 1.7 fusion.85
  116.8 1.9 collective-permute-start
  118.8 3.4 collective-permute-start.1
  122.1 2.6 collective-permute-done
  124.7 7.4 %collective-permute-done.1 = f32[5,4,2048]{2,1,0:T(4,128)S(1)} collective-permute-done((f32[5,4,2048]{2,1,0:T(4,128)S(1)}, f32[5,4,2048]{2,1,0:T(4,128)S(1)}, u32[]{:S(2)}, u32[]{:S(2)}) %collective-permute-start.1) | collective-permute-done | bytes 163872 | tf_op jit(solution)/shard_map/while/body/eval_jaxpr/ppermute | solution.py:26
  133.2 3.1 conditional.10
  137.5 1.9 collective-permute-start
  139.5 3.4 collective-permute-start.1
  143.6 7.4 %collective-permute-done.1 = f32[5,4,2048]{2,1,0:T(4,128)S(1)} collective-permute-done((f32[5,4,2048]{2,1,0:T(4,128)S(1)}, f32[5,4,2048]{2,1,0:T(4,128)S(1)}, u32[]{:S(2)}, u32[]{:S(2)}) %collective-permute-start.1) | collective-permute-done | bytes 163872 | tf_op jit(solution)/shard_map/while/body/eval_jaxpr/ppermute | solution.py:26
  152.1 3.1 conditional.10
  153.5 1.7 fusion.85
  156.4 1.9 collective-permute-start
  158.3 3.4 collective-permute-start.1
  162.5 7.4 %collective-permute-done.1 = f32[5,4,2048]{2,1,0:T(4,128)S(1)} collective-permute-done((f32[5,4,2048]{2,1,0:T(4,128)S(1)}, f32[5,4,2048]{2,1,0:T(4,128)S(1)}, u32[]{:S(2)}, u32[]{:S(2)}) %collective-permute-start.1) | collective-permute-done | bytes 163872 | tf_op jit(solution)/shard_map/while/body/eval_jaxpr/ppermute | solution.py:26
  170.9 3.1 conditional.10
  175.3 1.9 collective-permute-start
  177.2 3.4 collective-permute-start.1
  181.4 7.4 %collective-permute-done.1 = f32[5,4,2048]{2,1,0:T(4,128)S(1)} collective-permute-done((f32[5,4,2048]{2,1,0:T(4,128)S(1)}, f32[5,4,2048]{2,1,0:T(4,128)S(1)}, u32[]{:S(2)}, u32[]{:S(2)}) %collective-permute-start.1) | collective-permute-done | bytes 163872 | tf_op jit(solution)/shard_map/while/body/eval_jaxpr/ppermute | solution.py:26
  189.8 3.1 conditional.10
  193.7 6.0 %conditional.3 = (f32[3,32768]{0,1:T(8,128)}) conditional(s32[]{:T(128)} %convert_element_type.31, () %tuple.38, (s32[2,8,2048]{2,1,0:T(8,128)S(1)}, f32[3,8,2048]{2,1,0:T(8,128)}, s32[2,8,2048]{2,1,0:T(8,128)S(1)}) %tuple.122), branch_computations={%region_4.5_spmd, %region_5.7_spmd} | conditional | flops 262144 | bytes 2686988 | solution.py:201
  193.7 6.0 %broadcast.141 = f32[3,32768]{0,1:T(8,128)} broadcast(f32[]{:T(128)} %constant.39.clone), dimensions={} | broadcast | bytes 393220 | tf_op jit(solution)/shard_map/broadcast.49
  199.7 9.5 %copy.17 = f32[3,32768]{1,0:T(4,128)S(1)} copy(f32[3,32768]{0,1:T(8,128)} %get-tuple-element.427) | data formatting | bytes 786432 | tf_op jit(solution)/shard_map/cond | solution.py:201
  210.5 228.0 %collective-permute-done.4 = f32[3,32768]{1,0:T(4,128)S(1)} collective-permute-done((f32[3,32768]{1,0:T(4,128)S(1)}, f32[3,32768]{1,0:T(4,128)S(1)}, u32[]{:S(2)}, u32[]{:S(2)}) %collective-permute-start.4) | collective-permute-done | bytes 393248 | tf_op jit(solution)/shard_map/ppermute | solution.py:37
  438.5 1.9 collective-permute-start.5
  440.4 13.1 %collective-permute-done.5 = f32[3,16384]{1,0:T(4,128)S(1)} collective-permute-done((f32[3,16384]{1,0:T(4,128)S(1)}, f32[3,16384]{1,0:T(4,128)S(1)}, u32[]{:S(2)}, u32[]{:S(2)}) %collective-permute-start.5) | collective-permute-done | bytes 196640 | tf_op jit(solution)/shard_map/ppermute | solution.py:43
  453.6 3.7 conditional.4
  (106 shorter events, 53.7 us)
Async XLA Ops:
  4.4 25.1 %collective-permute-start.2 = (f32[8,4,2048]{2,1,0:T(4,128)S(1)}, f32[8,4,2048]{2,1,0:T(4,128)S(1)}, u32[]{:S(2)}, u32[]{:S(2)}) collective-permute-start(f32[8,4,2048]{2,1,0:T(4,128)S(1)} %get-tuple-element.305), channel_id=1, source_target_pairs={{0,1},{1,2},{2,3},{3,4},{4,5},{5,6},{6,7},{7,8},{8,9},{9,10},{10,1... | collective-permute-start | bytes 786440 | tf_op jit(solution)/shard_map/ppermute | solution.py:26
  7.5 22.9 %collective-permute-start.3 = (f32[8,4,2048]{2,1,0:T(4,128)S(1)}, f32[8,4,2048]{2,1,0:T(4,128)S(1)}, u32[]{:S(2)}, u32[]{:S(2)}) collective-permute-start(f32[8,4,2048]{2,1,0:T(4,128)S(1)} %get-tuple-element.306), channel_id=1, source_target_pairs={{1,0},{2,1},{3,2},{4,3},{5,4},{6,5},{7,6},{8,7},{9,8},{10,9},{11,1... | collective-permute-start | bytes 786440 | tf_op jit(solution)/shard_map/ppermute | solution.py:29
  32.5 161.2 %copy-start = (s32[2,8,2048]{2,1,0:T(8,128)S(1)}, s32[2,8,2048]{2,1,0:T(8,128)}, u32[]{:S(2)}) copy-start(s32[2,8,2048]{2,1,0:T(8,128)} %param.20) | copy-start | bytes 393220
  32.5 161.2 %copy-start.1 = (s32[2,8,2048]{2,1,0:T(8,128)S(1)}, s32[2,8,2048]{2,1,0:T(8,128)}, u32[]{:S(2)}) copy-start(s32[2,8,2048]{2,1,0:T(8,128)} %param.21) | copy-start | bytes 393220
  33.7 11.8 %collective-permute-start = (f32[5,4,2048]{2,1,0:T(4,128)S(1)}, f32[5,4,2048]{2,1,0:T(4,128)S(1)}, u32[]{:S(2)}, u32[]{:S(2)}) collective-permute-start(f32[5,4,2048]{2,1,0:T(4,128)S(1)} %get-tuple-element.374), channel_id=1, source_target_pairs={{1,0},{2,1},{3,2},{4,3},{5,4},{6,5},{7,6},{8,7},{9,8},{10,9},{11,1... | collective-permute-start | bytes 491528 | tf_op jit(solution)/shard_map/while/body/eval_jaxpr/ppermute | solution.py:29
  43.3 11.5 %collective-permute-start.1 = (f32[5,4,2048]{2,1,0:T(4,128)S(1)}, f32[5,4,2048]{2,1,0:T(4,128)S(1)}, u32[]{:S(2)}, u32[]{:S(2)}) collective-permute-start(f32[5,4,2048]{2,1,0:T(4,128)S(1)} %get-tuple-element.375), channel_id=1, source_target_pairs={{0,1},{1,2},{2,3},{3,4},{4,5},{5,6},{6,7},{7,8},{8,9},{9,10},{10,1... | collective-permute-start | bytes 491528 | tf_op jit(solution)/shard_map/while/body/eval_jaxpr/ppermute | solution.py:26
  60.2 6.1 %collective-permute-start = (f32[5,4,2048]{2,1,0:T(4,128)S(1)}, f32[5,4,2048]{2,1,0:T(4,128)S(1)}, u32[]{:S(2)}, u32[]{:S(2)}) collective-permute-start(f32[5,4,2048]{2,1,0:T(4,128)S(1)} %get-tuple-element.374), channel_id=1, source_target_pairs={{1,0},{2,1},{3,2},{4,3},{5,4},{6,5},{7,6},{8,7},{9,8},{10,9},{11,1... | collective-permute-start | bytes 491528 | tf_op jit(solution)/shard_map/while/body/eval_jaxpr/ppermute | solution.py:29
  62.1 11.5 %collective-permute-start.1 = (f32[5,4,2048]{2,1,0:T(4,128)S(1)}, f32[5,4,2048]{2,1,0:T(4,128)S(1)}, u32[]{:S(2)}, u32[]{:S(2)}) collective-permute-start(f32[5,4,2048]{2,1,0:T(4,128)S(1)} %get-tuple-element.375), channel_id=1, source_target_pairs={{0,1},{1,2},{2,3},{3,4},{4,5},{5,6},{6,7},{7,8},{8,9},{9,10},{10,1... | collective-permute-start | bytes 491528 | tf_op jit(solution)/shard_map/while/body/eval_jaxpr/ppermute | solution.py:26
  79.1 6.1 %collective-permute-start = (f32[5,4,2048]{2,1,0:T(4,128)S(1)}, f32[5,4,2048]{2,1,0:T(4,128)S(1)}, u32[]{:S(2)}, u32[]{:S(2)}) collective-permute-start(f32[5,4,2048]{2,1,0:T(4,128)S(1)} %get-tuple-element.374), channel_id=1, source_target_pairs={{1,0},{2,1},{3,2},{4,3},{5,4},{6,5},{7,6},{8,7},{9,8},{10,9},{11,1... | collective-permute-start | bytes 491528 | tf_op jit(solution)/shard_map/while/body/eval_jaxpr/ppermute | solution.py:29
  81.0 11.5 %collective-permute-start.1 = (f32[5,4,2048]{2,1,0:T(4,128)S(1)}, f32[5,4,2048]{2,1,0:T(4,128)S(1)}, u32[]{:S(2)}, u32[]{:S(2)}) collective-permute-start(f32[5,4,2048]{2,1,0:T(4,128)S(1)} %get-tuple-element.375), channel_id=1, source_target_pairs={{0,1},{1,2},{2,3},{3,4},{4,5},{5,6},{6,7},{7,8},{8,9},{9,10},{10,1... | collective-permute-start | bytes 491528 | tf_op jit(solution)/shard_map/while/body/eval_jaxpr/ppermute | solution.py:26
  98.0 6.4 %collective-permute-start = (f32[5,4,2048]{2,1,0:T(4,128)S(1)}, f32[5,4,2048]{2,1,0:T(4,128)S(1)}, u32[]{:S(2)}, u32[]{:S(2)}) collective-permute-start(f32[5,4,2048]{2,1,0:T(4,128)S(1)} %get-tuple-element.374), channel_id=1, source_target_pairs={{1,0},{2,1},{3,2},{4,3},{5,4},{6,5},{7,6},{8,7},{9,8},{10,9},{11,1... | collective-permute-start | bytes 491528 | tf_op jit(solution)/shard_map/while/body/eval_jaxpr/ppermute | solution.py:29
  99.9 11.5 %collective-permute-start.1 = (f32[5,4,2048]{2,1,0:T(4,128)S(1)}, f32[5,4,2048]{2,1,0:T(4,128)S(1)}, u32[]{:S(2)}, u32[]{:S(2)}) collective-permute-start(f32[5,4,2048]{2,1,0:T(4,128)S(1)} %get-tuple-element.375), channel_id=1, source_target_pairs={{0,1},{1,2},{2,3},{3,4},{4,5},{5,6},{6,7},{7,8},{8,9},{9,10},{10,1... | collective-permute-start | bytes 491528 | tf_op jit(solution)/shard_map/while/body/eval_jaxpr/ppermute | solution.py:26
  116.8 7.9 %collective-permute-start = (f32[5,4,2048]{2,1,0:T(4,128)S(1)}, f32[5,4,2048]{2,1,0:T(4,128)S(1)}, u32[]{:S(2)}, u32[]{:S(2)}) collective-permute-start(f32[5,4,2048]{2,1,0:T(4,128)S(1)} %get-tuple-element.374), channel_id=1, source_target_pairs={{1,0},{2,1},{3,2},{4,3},{5,4},{6,5},{7,6},{8,7},{9,8},{10,9},{11,1... | collective-permute-start | bytes 491528 | tf_op jit(solution)/shard_map/while/body/eval_jaxpr/ppermute | solution.py:29
  118.8 13.3 %collective-permute-start.1 = (f32[5,4,2048]{2,1,0:T(4,128)S(1)}, f32[5,4,2048]{2,1,0:T(4,128)S(1)}, u32[]{:S(2)}, u32[]{:S(2)}) collective-permute-start(f32[5,4,2048]{2,1,0:T(4,128)S(1)} %get-tuple-element.375), channel_id=1, source_target_pairs={{0,1},{1,2},{2,3},{3,4},{4,5},{5,6},{6,7},{7,8},{8,9},{9,10},{10,1... | collective-permute-start | bytes 491528 | tf_op jit(solution)/shard_map/while/body/eval_jaxpr/ppermute | solution.py:26
  137.5 6.1 %collective-permute-start = (f32[5,4,2048]{2,1,0:T(4,128)S(1)}, f32[5,4,2048]{2,1,0:T(4,128)S(1)}, u32[]{:S(2)}, u32[]{:S(2)}) collective-permute-start(f32[5,4,2048]{2,1,0:T(4,128)S(1)} %get-tuple-element.374), channel_id=1, source_target_pairs={{1,0},{2,1},{3,2},{4,3},{5,4},{6,5},{7,6},{8,7},{9,8},{10,9},{11,1... | collective-permute-start | bytes 491528 | tf_op jit(solution)/shard_map/while/body/eval_jaxpr/ppermute | solution.py:29
  139.5 11.5 %collective-permute-start.1 = (f32[5,4,2048]{2,1,0:T(4,128)S(1)}, f32[5,4,2048]{2,1,0:T(4,128)S(1)}, u32[]{:S(2)}, u32[]{:S(2)}) collective-permute-start(f32[5,4,2048]{2,1,0:T(4,128)S(1)} %get-tuple-element.375), channel_id=1, source_target_pairs={{0,1},{1,2},{2,3},{3,4},{4,5},{5,6},{6,7},{7,8},{8,9},{9,10},{10,1... | collective-permute-start | bytes 491528 | tf_op jit(solution)/shard_map/while/body/eval_jaxpr/ppermute | solution.py:26
  156.4 6.1 %collective-permute-start = (f32[5,4,2048]{2,1,0:T(4,128)S(1)}, f32[5,4,2048]{2,1,0:T(4,128)S(1)}, u32[]{:S(2)}, u32[]{:S(2)}) collective-permute-start(f32[5,4,2048]{2,1,0:T(4,128)S(1)} %get-tuple-element.374), channel_id=1, source_target_pairs={{1,0},{2,1},{3,2},{4,3},{5,4},{6,5},{7,6},{8,7},{9,8},{10,9},{11,1... | collective-permute-start | bytes 491528 | tf_op jit(solution)/shard_map/while/body/eval_jaxpr/ppermute | solution.py:29
  158.3 11.5 %collective-permute-start.1 = (f32[5,4,2048]{2,1,0:T(4,128)S(1)}, f32[5,4,2048]{2,1,0:T(4,128)S(1)}, u32[]{:S(2)}, u32[]{:S(2)}) collective-permute-start(f32[5,4,2048]{2,1,0:T(4,128)S(1)} %get-tuple-element.375), channel_id=1, source_target_pairs={{0,1},{1,2},{2,3},{3,4},{4,5},{5,6},{6,7},{7,8},{8,9},{9,10},{10,1... | collective-permute-start | bytes 491528 | tf_op jit(solution)/shard_map/while/body/eval_jaxpr/ppermute | solution.py:26
  175.3 6.1 %collective-permute-start = (f32[5,4,2048]{2,1,0:T(4,128)S(1)}, f32[5,4,2048]{2,1,0:T(4,128)S(1)}, u32[]{:S(2)}, u32[]{:S(2)}) collective-permute-start(f32[5,4,2048]{2,1,0:T(4,128)S(1)} %get-tuple-element.374), channel_id=1, source_target_pairs={{1,0},{2,1},{3,2},{4,3},{5,4},{6,5},{7,6},{8,7},{9,8},{10,9},{11,1... | collective-permute-start | bytes 491528 | tf_op jit(solution)/shard_map/while/body/eval_jaxpr/ppermute | solution.py:29
  177.2 11.5 %collective-permute-start.1 = (f32[5,4,2048]{2,1,0:T(4,128)S(1)}, f32[5,4,2048]{2,1,0:T(4,128)S(1)}, u32[]{:S(2)}, u32[]{:S(2)}) collective-permute-start(f32[5,4,2048]{2,1,0:T(4,128)S(1)} %get-tuple-element.375), channel_id=1, source_target_pairs={{0,1},{1,2},{2,3},{3,4},{4,5},{5,6},{6,7},{7,8},{8,9},{9,10},{10,1... | collective-permute-start | bytes 491528 | tf_op jit(solution)/shard_map/while/body/eval_jaxpr/ppermute | solution.py:26
  209.2 229.3 %collective-permute-start.4 = (f32[3,32768]{1,0:T(4,128)S(1)}, f32[3,32768]{1,0:T(4,128)S(1)}, u32[]{:S(2)}, u32[]{:S(2)}) collective-permute-start(f32[3,32768]{1,0:T(4,128)S(1)} %copy.17), channel_id=1, source_target_pairs={{0,512},{1,513},{2,514},{3,515},{4,516},{5,517},{6,518},{7,519},{8... | collective-permute-start | bytes 1179656 | tf_op jit(solution)/shard_map/ppermute | solution.py:37
  438.5 15.1 %collective-permute-start.5 = (f32[3,16384]{1,0:T(4,128)S(1)}, f32[3,16384]{1,0:T(4,128)S(1)}, u32[]{:S(2)}, u32[]{:S(2)}) collective-permute-start(f32[3,16384]{1,0:T(4,128)S(1)} %slice.432), channel_id=1, source_target_pairs={{0,1},{1,2},{2,3},{3,4},{4,5},{5,6},{6,7},{7,8},{8,9},{9,10},{10,1... | collective-permute-start | bytes 589832 | tf_op jit(solution)/shard_map/ppermute | solution.py:43
where the time goes:
time: 460 us; the launch traced here: 457 us
  waiting for transfers between devices  314 us (68%)
  starting transfers between devices  72.7 us (16%)
  other arithmetic  39.1 us (8%)
  local copies, waits for them, and re-layouts  29.5 us (6%)
    ppermute x1, waiting for transfers between devices, shifted(): lax.ppermute(value, axis, [(source, source + steps) for source in range(f...  228 us
    ppermute x9, waiting for transfers between devices, extended_2(): lax.ppermute(lax.slice_in_dim(block, block.shape[dim] - width, None, axis...  64.5 us
    ppermute x9, starting transfers between devices, extended_2(): lax.ppermute(lax.slice_in_dim(block, 0, width, axis=dim), axis, backward)  40.9 us
    ppermute x9, starting transfers between devices, extended_2(): lax.ppermute(lax.slice_in_dim(block, block.shape[dim] - width, None, axis...  28.6 us
    sub x16, other arithmetic, ocean_step(): return centre - courant * change  23.4 us
    ppermute x1, waiting for transfers between devices, from_behind(): return lax.ppermute(value, axis, pairs)  13.1 us
    concatenate x9, other arithmetic, extended_2(): block = jnp.concatenate([low, block, high], axis=dim)  9.76 us
    cond x1, local copies, waits for them, and re-layouts, body(): partial_sums = lax.cond(is_ice, window_sums, no_window, average)  9.46 us
  transfers between devices with their start and end apart: 20, of which 20 were waited for; matrix products, arithmetic and copies ran while one was open for 0% of the time, Pallas kernels for 0%

commit v1 on v0

v1 whole, which is shorter than its diff:
```python
import jax
import jax.numpy as jnp
from jax import lax
from jax.experimental import pallas as pl
from jax.experimental.pallas import tpu as pltpu
from jax.sharding import PartitionSpec as P

SUBCYCLES = 16
ICE_DEPTH = 4
OCEAN_DEPTH = 8
LANES = 128
PAD = 8
GROUP = 4

keep = 1.0 / 1.5
gain = 0.5 / 1.5
coriolis = 0.1
drag_coef = 1.0
inertia = 4.0
courant = 0.2
dilution = 0.5
weight_norm = 4.0
level_speed = (1.0, 0.8, 0.6, 0.45, 0.3)

VMEM = pl.BlockSpec(memory_space=pltpu.VMEM)
SMEM = pl.BlockSpec(memory_space=pltpu.SMEM)
LIMITED = pltpu.CompilerParams(vmem_limit_bytes=20 * 1024 * 1024)


def prep_kernel(flag, initial, forcing, current, cover, out):
    @pl.when(flag[0] == 0)
    def _():
        out[0] = initial[0, 0]
        out[1] = initial[0, 1]
        out[2] = initial[0, 2] + initial[0, 3]
        out[3] = initial[0, 2] - initial[0, 3]
        out[4] = 2.0 * initial[0, 4]
        covered = cover[...].astype(jnp.float32)
        out[5] = gain * forcing[1] * covered
        g = covered / (inertia * forcing[0] + drag_coef)
        out[6] = g
        out[7] = g * (forcing[2] + drag_coef * current[0])
        out[8] = g * (forcing[3] + drag_coef * current[1])

    @pl.when(flag[0] != 0)
    def _():
        for level in range(5):
            out[level] = initial[0, level]
        out[5] = current[0]
        out[6] = current[1]
        out[7] = jnp.zeros_like(current[0])
        out[8] = jnp.zeros_like(current[0])


def load_window(dst, dst_plane, src_plane, low, own, high, tiles, base):
    rows = own.shape[1]
    for part, ref in enumerate((low, own, high)):
        for c in range(tiles):
            dst[dst_plane, base[1] + c, pl.ds(base[0] + part * rows, rows), :] = ref[
                src_plane, :, c * LANES : (c + 1) * LANES
            ]


def make_round(first, last, ocean_active, rows, tiles):
    window = 3 * rows
    low_off = PAD

    def spans(margin):
        count = window - 2 * margin
        if count <= 8:
            return (8,)
        if count <= 16:
            return (4, 12)
        return (0, 8, 16)

    def kernel(*refs):
        refs = list(refs)
        flag = refs.pop(0)
        own, low, high = refs[:3]
        refs = refs[3:]
        if not first:
            stat, total_in = refs[:2]
            refs = refs[2:]
        if last:
            melt, current, cover = refs[:3]
            refs = refs[3:]
        if first:
            out, total, stat = refs[:3]
            refs = refs[3:]
        else:
            out, total = refs[:2]
            refs = refs[2:]
        field, other = refs

        lane = lax.broadcasted_iota(jnp.int32, (8, LANES), 1)
        at_first = lane == 0
        at_last = lane == LANES - 1
        zero_column = jnp.zeros((window + 2 * PAD, LANES), jnp.float32)

        def sides(ref, plane, column, row, cache):
            def rolled(c, shift):
                key = (plane, c, row, shift)
                if key not in cache:
                    tile = ref[plane, column[c], pl.ds(row, 8), :]
                    cache[key] = pltpu.roll(tile, shift, 1)
                return cache[key]

            def at(i):
                left = jnp.where(at_first, rolled(i, 1), rolled(i + 1, 1))
                right = jnp.where(at_last, rolled(i + 2, LANES - 1), rolled(i + 1, LANES - 1))
                return left, right

            return at

        def over_tiles(body):
            def step(group, carry):
                column = [group * GROUP + i for i in range(GROUP + 2)]
                body(group, column)
                return carry

            lax.fori_loop(0, tiles // GROUP, step, 0)

        def ice():
            if first:
                for plane in range(4):
                    load_window(stat, plane, 5 + plane, low, own, high, tiles, (0, 0))
                for part in range(3):
                    total[part] = jnp.zeros((rows, tiles * LANES), jnp.float32)
            else:
                for part in range(3):
                    total[part] = total_in[part]
            for plane in range(5):
                load_window(field, plane, plane, low, own, high, tiles, (low_off, 1))
                field[plane, 0] = zero_column
                field[plane, tiles + 1] = zero_column

            for turn in range(ICE_DEPTH):
                stress_spans = spans(2 * turn + 1)
                speed_spans = spans(2 * turn + 2)

                def stress(group, column):
                    for span in stress_spans:
                        row = span + low_off
                        cache = {}
                        side_x = sides(field, 0, column, row, cache)
                        side_y = sides(field, 1, column, row, cache)
                        for i in range(GROUP):
                            here = column[i + 1]
                            left_x, right_x = side_x(i)
                            left_y, right_y = side_y(i)
                            row_x = (
                                field[0, here, pl.ds(row + 1, 8), :]
                                - field[0, here, pl.ds(row - 1, 8), :]
                            )
                            row_y = (
                                field[1, here, pl.ds(row + 1, 8), :]
                                - field[1, here, pl.ds(row - 1, 8), :]
                            )
                            col_x = right_x - left_x
                            col_y = right_y - left_y
                            strain_d = row_x + col_y
                            strain_t = row_x - col_y
                            strain_s = col_x + row_y
                            quarter_t = 0.25 * strain_t
                            square = (
                                strain_d * strain_d
                                + quarter_t * strain_t
                                + 0.25 * (strain_s * strain_s)
                                + 0.04
                            )
                            press = stat[0, column[i], pl.ds(span, 8), :]
                            scaled = press * lax.rsqrt(square)
                            at = (here, pl.ds(row, 8), slice(None))
                            field[(2,) + at] = keep * field[(2,) + at] + (
                                scaled * (strain_d + quarter_t) - press
                            )
                            field[(3,) + at] = keep * field[(3,) + at] + (
                                scaled * (strain_d - quarter_t) - press
                            )
                            field[(4,) + at] = keep * field[(4,) + at] + scaled * (
                                0.25 * strain_s
                            )

                def speed(group, column):
                    for span in speed_spans:
                        row = span + low_off
                        cache = {}
                        side_q = sides(field, 4, column, row, cache)
                        side_m = sides(field, 3, column, row, cache)
                        for i in range(GROUP):
                            here = column[i + 1]
                            left_q, right_q = side_q(i)
                            left_m, right_m = side_m(i)
                            force_x = (
                                field[2, here, pl.ds(row + 1, 8), :]
                                - field[2, here, pl.ds(row - 1, 8), :]
                            ) + (right_q - left_q)
                            force_y = (
                                field[4, here, pl.ds(row + 1, 8), :]
                                - field[4, here, pl.ds(row - 1, 8), :]
                            ) + (right_m - left_m)
                            at = (here, pl.ds(row, 8), slice(None))
                            old_x = field[(0,) + at]
                            old_y = field[(1,) + at]
                            beside = (column[i], pl.ds(span, 8), slice(None))
                            g = stat[(1,) + beside]
                            held = jnp.where(g > 0.0, 1.0 - g, 0.0)
                            quarter = 0.25 * g
                            field[(0,) + at] = (
                                held * (old_x + coriolis * old_y)
                                + quarter * force_x
                                + stat[(2,) + beside]
                            )
                            field[(1,) + at] = (
                                held * (old_y - coriolis * old_x)
                                + quarter * force_y
                                + stat[(3,) + beside]
                            )
                    for i in range(GROUP):
                        here = column[i + 1]
                        new_x = field[0, here, pl.ds(rows + low_off, 8), :]
                        new_y = field[1, here, pl.ds(rows + low_off, 8), :]
                        lanes = pl.ds(pl.multiple_of(column[i] * LANES, LANES), LANES)
                        total[0, :, lanes] += new_x
                        total[1, :, lanes] += new_y
                        total[2, :, lanes] += jnp.sqrt(1.0 + new_x * new_x + new_y * new_y)

                over_tiles(stress)
                over_tiles(speed)

            for c in range(tiles):
                lanes = slice(c * LANES, (c + 1) * LANES)
                mine = [field[p, c + 1, low_off + rows : low_off + 2 * rows, :] for p in range(5)]
                if last:
                    mine[2:] = [
                        0.5 * (mine[2] + mine[3]),
                        0.5 * (mine[2] - mine[3]),
                        0.5 * mine[4],
                    ]
                    covered = cover[:, lanes].astype(jnp.float32)
                    total[0, :, lanes] = (
                        total[0, :, lanes] * (1.0 / SUBCYCLES) - covered * current[0, :, lanes]
                    )
                    total[1, :, lanes] = (
                        total[1, :, lanes] * (1.0 / SUBCYCLES) - covered * current[1, :, lanes]
                    )
                    total[2, :, lanes] = (
                        total[2, :, lanes] * (melt[0, :, lanes] * covered) * (1.0 / SUBCYCLES)
                    )
                for p in range(5):
                    out[p, :, lanes] = mine[p]

        def ocean():
            if first:
                for plane in range(2):
                    load_window(stat, plane, 5 + plane, low, own, high, tiles, (0, 0))
            if not ocean_active:
                out[...] = own[:5]
                return
            for plane in range(5):
                load_window(field, plane, plane, low, own, high, tiles, (low_off, 1))
                for ref in (field, other):
                    ref[plane, 0] = zero_column
                    ref[plane, tiles + 1] = zero_column

            for turn in range(OCEAN_DEPTH):
                source, target = (field, other) if turn % 2 == 0 else (other, field)
                row_spans = spans(turn + 1)

                def advect(group, column):
                    for span in row_spans:
                        row = span + low_off
                        pos_x, neg_x, pos_y, neg_y = [], [], [], []
                        for i in range(GROUP):
                            beside = (column[i], pl.ds(span, 8), slice(None))
                            ux = courant * stat[(0,) + beside]
                            uy = courant * stat[(1,) + beside]
                            pos_x.append(jnp.maximum(ux, 0.0))
                            neg_x.append(jnp.minimum(ux, 0.0))
                            pos_y.append(jnp.maximum(uy, 0.0))
                            neg_y.append(jnp.minimum(uy, 0.0))
                        for level in range(5):
                            side = sides(source, level, column, row, {})
                            for i in range(GROUP):
                                here = column[i + 1]
                                left, right = side(i)
                                centre = source[level, here, pl.ds(row, 8), :]
                                below = source[level, here, pl.ds(row - 1, 8), :]
                                above = source[level, here, pl.ds(row + 1, 8), :]
                                change = (
                                    pos_x[i] * (centre - below)
                                    + neg_x[i] * (above - centre)
                                    + pos_y[i] * (centre - left)
                                    + neg_y[i] * (right - centre)
                                )
                                if level:
                                    change = level_speed[level] * change
                                target[level, here, pl.ds(row, 8), :] = centre - change

                over_tiles(advect)

            done = field if OCEAN_DEPTH % 2 == 0 else other
            for p in range(5):
                for c in range(tiles):
                    out[p, :, c * LANES : (c + 1) * LANES] = done[
                        p, c + 1, low_off + rows : low_off + 2 * rows, :
                    ]

        @pl.when(flag[0] == 0)
        def _():
            ice()

        @pl.when(flag[0] != 0)
        def _():
            ocean()

    return kernel


HIGH = 64
WIDE = 256


def scatter_half(half, values, targets, weights, out, left, right, sums):
    rows = values.shape[1]
    columns = values.shape[2]
    groups = columns // WIDE
    spots = rows * groups
    sums[...] = jnp.zeros_like(sums)
    high_at = lax.broadcasted_iota(jnp.int32, (spots, columns), 0).astype(jnp.bfloat16)
    low_at = lax.broadcasted_iota(jnp.int32, (WIDE, columns), 0).astype(jnp.bfloat16)
    zero = jnp.zeros((), jnp.bfloat16)
    one = jnp.ones((), jnp.bfloat16)

    def step(turn, carry):
        entry = turn // rows
        row = turn % rows
        spot = targets[entry, pl.ds(row, 1), :]
        scale = weights[entry, pl.ds(row, 1), :].astype(jnp.float32) / weight_norm
        low = jnp.bitwise_and(spot, WIDE - 1)
        high = jnp.right_shift(spot, 8) - half * spots
        inside = jnp.logical_and(high >= 0, high < spots)
        place = jnp.bitwise_and(high, groups - 1) * rows + high // groups
        place = jnp.where(inside, place, -1)
        low = low.astype(jnp.float32).astype(jnp.bfloat16)
        place = place.astype(jnp.float32).astype(jnp.bfloat16)
        right[...] = jnp.where(low_at == low, one, zero)
        hit = high_at == place
        for channel in range(3):
            value = values[channel, pl.ds(row, 1), :] * scale
            coarse = value.astype(jnp.bfloat16)
            fine = (value - coarse.astype(jnp.float32)).astype(jnp.bfloat16)
            left[2 * channel * spots : (2 * channel + 1) * spots, :] = jnp.where(hit, coarse, zero)
            left[(2 * channel + 1) * spots : (2 * channel + 2) * spots, :] = jnp.where(
                hit, fine, zero
            )
        sums[...] += lax.dot_general(
            left[...],
            right[...],
            (((1,), (1,)), ((), ())),
            preferred_element_type=jnp.float32,
        )
        return carry

    lax.fori_loop(0, 2 * rows, step, 0)
    for channel in range(3):
        for g in range(groups):
            first = 2 * channel * spots + g * rows
            second = first + spots
            out[channel, :, g * WIDE : (g + 1) * WIDE] = (
                sums[first : first + rows, :] + sums[second : second + rows, :]
            )


def upper_kernel(flag, average, targets, weights, out, left, right, sums):
    @pl.when(flag[0] == 0)
    def _():
        scatter_half(1, average, targets, weights, out, left, right, sums)


def lower_kernel(flag, average, targets, weights, out, left, right, sums):
    @pl.when(flag[0] != 0)
    def _():
        scatter_half(0, average, targets, weights, out, left, right, sums)


def final_kernel(flag, fields, average, lower, upper, state, coupled):
    @pl.when(flag[0] == 0)
    def _():
        state[0] = fields[...]
        coupled[0] = average[...]

    @pl.when(flag[0] != 0)
    def _():
        flux = lower[...] + upper[...]
        coupled[0] = flux
        state[0, 0] = fields[0] - dilution * flux[2]
        state[0, 1:] = fields[1:]


def body(initial, ice_forcing, ocean_current, ice_cover, targets, weights):
    rows, columns = initial.shape[2:]
    tiles = columns // LANES
    strips = lax.axis_size("blk")
    flag = lax.axis_index("comp").astype(jnp.int32).reshape(1)
    both = ("comp", "blk")

    def moved(value, kinds, step):
        pairs = [
            (kind * strips + b, kind * strips + b + step)
            for kind in kinds
            for b in range(strips)
            if 0 <= b + step < strips
        ]
        return lax.ppermute(value, both, pairs)

    def shape(*dims):
        return pltpu.VMEM(dims, jnp.float32)

    def held(*values):
        return [pltpu.with_memory_space_constraint(value, pltpu.VMEM) for value in values]

    block = pl.pallas_call(
        prep_kernel,
        compiler_params=LIMITED,
        out_shape=shape(9, rows, columns),
        in_specs=[SMEM] + [VMEM] * 4,
        out_specs=VMEM,
    )(flag, initial, ice_forcing, ocean_current, ice_cover)

    rounds = SUBCYCLES // ICE_DEPTH
    each = OCEAN_DEPTH // ICE_DEPTH
    window = 3 * rows
    stat = total = None
    for turn in range(rounds):
        first, last = turn == 0, turn == rounds - 1
        active = turn % each == 0
        kinds = (0, 1) if active else (0,)
        low = moved(block, kinds, 1)
        high = moved(block, kinds, -1)
        operands = [flag, block, low, high]
        outs = [shape(5, rows, columns), shape(3, rows, columns)]
        if not first:
            operands += [stat, total]
        if last:
            operands += [ice_forcing[4:], ocean_current, ice_cover]
        if first:
            outs.append(shape(4, tiles, window, LANES))
        done = pl.pallas_call(
            make_round(first, last, active, rows, tiles),
            compiler_params=LIMITED,
            out_shape=outs,
            in_specs=[SMEM] + [VMEM] * (len(operands) - 1),
            out_specs=[VMEM] * len(outs),
            scratch_shapes=[pltpu.VMEM((5, tiles + 2, window + 2 * PAD, LANES), jnp.float32)] * 2,
        )(flag, *held(*operands[1:]))
        block, total = done[:2]
        if first:
            stat = done[2]

    average = total
    scatter_scratch = [
        pltpu.VMEM((6 * rows * columns // WIDE, columns), jnp.bfloat16),
        pltpu.VMEM((WIDE, columns), jnp.bfloat16),
        pltpu.VMEM((6 * rows * columns // WIDE, WIDE), jnp.float32),
    ]

    def scattered(kernel, values):
        return pl.pallas_call(
            kernel,
            compiler_params=LIMITED,
            out_shape=shape(3, rows, columns),
            in_specs=[SMEM] + [VMEM] * 3,
            out_specs=VMEM,
            scratch_shapes=scatter_scratch,
        )(flag, *held(values, targets, weights))

    received = lax.ppermute(average, both, [(b, strips + b) for b in range(strips)])
    upper = scattered(upper_kernel, average)
    beyond = lax.ppermute(upper, both, [(b, strips + (b + 1) % strips) for b in range(strips)])
    lower = scattered(lower_kernel, received)
    return tuple(
        pl.pallas_call(
            final_kernel,
            compiler_params=LIMITED,
            out_shape=[
                jax.ShapeDtypeStruct((1, 5, rows, columns), jnp.float32),
                jax.ShapeDtypeStruct((1, 3, rows, columns), jnp.float32),
            ],
            in_specs=[SMEM] + [VMEM] * 4,
            out_specs=[VMEM] * 2,
        )(flag, *held(block, average, lower, beyond))
    )


def solution(mesh):
    placed = (
        P("comp", None, "blk", None),
        P(None, "blk", None),
        P(None, "blk", None),
        P("blk", None),
        P(None, "blk", None),
        P(None, "blk", None),
    )
    return jax.shard_map(
        body,
        mesh=mesh,
        in_specs=placed,
        out_specs=(P("comp", None, "blk", None), P("comp", None, "blk", None)),
        check_vma=False,
    )
```

time: 460 us -> 133 us (0.29)
  waiting for transfers between devices: 314 us -> 65.5 us
  other arithmetic: 39.1 us -> 0 us
  starting transfers between devices: 72.7 us -> 38.1 us
  local copies, waits for them, and re-layouts: 29.5 us -> 4.55 us
  Pallas kernels: 0 us -> 23.7 us
    ppermute x20 -> x10, waiting for transfers between devices: 314 us -> 65.5 us  [the longest x1 36 us: body(): lax.ppermute(average, both, [(b, strips + b) for b in range(strips)])]
    ppermute x20 -> x10, starting transfers between devices: 72.7 us -> 38.1 us  [the longest x8 35.4 us: moved(): return lax.ppermute(value, both, pairs)]
    sub x17 -> x0, other arithmetic: 24.2 us -> none  [the longest x16 23.4 us: ocean_step(): return centre - courant * change]
    pallas_call x0 -> x8, Pallas kernels: none -> 23.7 us  [the longest x4 12.8 us: body(): pl.pallas_call(make_round(first, last, active, rows, tiles), compiler_par...]
    concatenate x10 -> x0, other arithmetic: 10.8 us -> none  [the longest x9 9.76 us: extended_2(): block = jnp.concatenate([low, block, high], axis=dim)]
    cond x2 -> x0, local copies, waits for them, and re-layouts: 10.3 us -> none  [the longest x1 9.46 us: body(): partial_sums = lax.cond(is_ice, window_sums, no_window, average)]
    slice x27 -> x1, local copies, waits for them, and re-layouts: 11.1 us -> 0.85 us  [body(): operands += [ice_forcing[4:], ocean_current, ice_cover]]
    another operation x1 -> x0, local copies, waits for them, and re-layouts: 6.01 us -> none
  transfers between devices with their start and end apart: 20 -> 10, of which waited for: 20 -> 6; matrix products, arithmetic and copies ran while one was open for 0% -> 1% of each run, Pallas kernels for 0% -> 8%
where the time goes in v1:
time: 133 us
  waiting for transfers between devices  65.5 us (49%)
  starting transfers between devices  38.1 us (29%)
  Pallas kernels  23.7 us (18%)
  local copies, waits for them, and re-layouts  4.55 us (3%)
    ppermute x1, waiting for transfers between devices, body(): lax.ppermute(average, both, [(b, strips + b) for b in range(strips)])  36 us
    ppermute x8, starting transfers between devices, moved(): return lax.ppermute(value, both, pairs)  35.4 us
    ppermute x8, waiting for transfers between devices, moved(): return lax.ppermute(value, both, pairs)  18.2 us
    pallas_call x4, Pallas kernels, body(): pl.pallas_call(make_round(first, last, active, rows, tiles), compiler_par...  12.8 us
    ppermute x1, waiting for transfers between devices, body(): lax.ppermute(upper, both, [(b, strips + (b + 1) % strips) for b in range(...  11.3 us
    pallas_call x2, Pallas kernels, scattered(): pl.pallas_call(kernel, compiler_params=LIMITED, out_shape=shape(3, rows,...  10 us
    unnamed x16, local copies, waits for them, and re-layouts  3.71 us
  transfers between devices with their start and end apart: 10, of which 6 were waited for; matrix products, arithmetic and copies ran while one was open for 1% of the time, Pallas kernels for 8%

profile of v1, /device:TPU:65, one launch (start us, length us, event | category | flops | bytes accessed | tf_op | source)
XLA Modules:
  0.0 132.7 jit_solution(11334188027696690021)
XLA Ops:
  0.6 0.0 copy-start
  0.6 0.9 copy-done
  1.5 0.0 copy-start.4
  1.5 1.0 copy-done.4
  2.5 0.0 copy-start.5
  2.5 1.0 copy-done.5
  3.5 0.0 copy-start.6
  3.5 0.8 copy-done.6
  4.4 3.1 %collective-permute-start = (f32[9,8,2048]{2,1,0:T(8,128)S(1)}, f32[9,8,2048]{2,1,0:T(8,128)S(1)}, u32[]{:S(2)}, u32[]{:S(2)}) collective-permute-start(f32[9,8,2048]{2,1,0:T(8,128)S(1)} %shard_map.77.refs_1_), channel_id=1, source_target_pairs={{0,1},{1,2},{2,3},{3,4},{4,5},{5,6},{6,7},{7,8},{8,9},{9,10},{10,1... | collective-permute-start | bytes 1769480 | tf_op jit(solution)/shard_map/ppermute | solution.py:415
  7.5 17.9 %collective-permute-start.1 = (f32[9,8,2048]{2,1,0:T(8,128)S(1)}, f32[9,8,2048]{2,1,0:T(8,128)S(1)}, u32[]{:S(2)}, u32[]{:S(2)}) collective-permute-start(f32[9,8,2048]{2,1,0:T(8,128)S(1)} %shard_map.77.refs_1_), channel_id=1, source_target_pairs={{1,0},{2,1},{3,2},{4,3},{5,4},{6,5},{7,6},{8,7},{9,8},{10,9},{11,1... | collective-permute-start | bytes 1769480 | tf_op jit(solution)/shard_map/ppermute | solution.py:415
  25.4 11.1 %collective-permute-done.refs_2_ = f32[9,8,2048]{2,1,0:T(8,128)S(1)} collective-permute-done((f32[9,8,2048]{2,1,0:T(8,128)S(1)}, f32[9,8,2048]{2,1,0:T(8,128)S(1)}, u32[]{:S(2)}, u32[]{:S(2)}) %collective-permute-start) | collective-permute-done | bytes 589856 | tf_op jit(solution)/shard_map/ppermute | solution.py:415
  36.5 0.9 collective-permute-done.1.refs_3_
  37.4 6.4 %shard_map.78 = (f32[5,8,2048]{2,1,0:T(8,128)S(1)}, f32[3,8,2048]{2,1,0:T(8,128)S(1)}, f32[4,16,24,128]{3,2,1,0:T(8,128)S(1)}) custom-call(s32[1]{0:T(128)} %bitcast.flag.refs_0_, f32[9,8,2048]{2,1,0:T(8,128)S(1)} %shard_map.77.refs_1_, f32[9,8,2048]{2,1,0:T(8,128)S(1)} %collective-permute-done.refs_2_, f32[9,8,2048]{2,1,0:T(8,128)S(1)} %collective-permute-done.1.refs_3_), custom_call_target="tpu_custom_call" | custom-call | tf_op jit(solution)/shard_map/pallas_call | solution.py:449
  43.8 0.7 collective-permute-start.2
  44.5 0.7 collective-permute-start.3
  45.2 0.0 collective-permute-done.2.refs_2_
  45.2 0.0 collective-permute-done.3.refs_3_
  45.2 1.9 %collective-permute-start.4 = (f32[5,8,2048]{2,1,0:T(8,128)S(1)}, f32[5,8,2048]{2,1,0:T(8,128)S(1)}, u32[]{:S(2)}, u32[]{:S(2)}) collective-permute-start(f32[5,8,2048]{2,1,0:T(8,128)S(1)} %get-tuple-element.14.refs_1_), channel_id=1, source_target_pairs={{0,1},{1,2},{2,3},{3,4},{4,5},{5,6},{6,7},{7,8},{8,9},{9,10},{10,1... | collective-permute-start | bytes 983048 | tf_op jit(solution)/shard_map/ppermute | solution.py:415
  47.2 9.5 %collective-permute-start.5 = (f32[5,8,2048]{2,1,0:T(8,128)S(1)}, f32[5,8,2048]{2,1,0:T(8,128)S(1)}, u32[]{:S(2)}, u32[]{:S(2)}) collective-permute-start(f32[5,8,2048]{2,1,0:T(8,128)S(1)} %get-tuple-element.14.refs_1_), channel_id=1, source_target_pairs={{1,0},{2,1},{3,2},{4,3},{5,4},{6,5},{7,6},{8,7},{9,8},{10,9},{11,1... | collective-permute-start | bytes 983048 | tf_op jit(solution)/shard_map/ppermute | solution.py:415
  56.7 4.5 %collective-permute-done.4.refs_2_ = f32[5,8,2048]{2,1,0:T(8,128)S(1)} collective-permute-done((f32[5,8,2048]{2,1,0:T(8,128)S(1)}, f32[5,8,2048]{2,1,0:T(8,128)S(1)}, u32[]{:S(2)}, u32[]{:S(2)}) %collective-permute-start.4) | collective-permute-done | bytes 327712 | tf_op jit(solution)/shard_map/ppermute | solution.py:415
  61.2 1.8 %collective-permute-done.5.refs_3_ = f32[5,8,2048]{2,1,0:T(8,128)S(1)} collective-permute-done((f32[5,8,2048]{2,1,0:T(8,128)S(1)}, f32[5,8,2048]{2,1,0:T(8,128)S(1)}, u32[]{:S(2)}, u32[]{:S(2)}) %collective-permute-start.5) | collective-permute-done | bytes 327712 | tf_op jit(solution)/shard_map/ppermute | solution.py:415
  62.9 0.0 copy-start.7
  62.9 6.4 %shard_map.80 = (f32[5,8,2048]{2,1,0:T(8,128)S(1)}, f32[3,8,2048]{2,1,0:T(8,128)S(1)}) custom-call(s32[1]{0:T(128)} %bitcast.flag.refs_0_, f32[5,8,2048]{2,1,0:T(8,128)S(1)} %get-tuple-element.14.refs_1_, f32[5,8,2048]{2,1,0:T(8,128)S(1)} %collective-permute-done.4.refs_2_, f32[5,8,2048]{2,1,0:T(8,128)S(1)} %collective-permute-done.5.refs_3_, ...), custom_call_target="tpu_custom_call" | custom-call | tf_op jit(solution)/shard_map/pallas_call | solution.py:449
  69.3 0.0 copy-start.1
  69.3 0.8 collective-permute-start.6
  70.1 0.7 collective-permute-start.7
  70.8 0.8 slice.3.refs_6_
  71.7 0.0 collective-permute-done.6.refs_2_
  71.7 0.0 collective-permute-done.7.refs_3_
  71.7 0.0 copy-done.7
  71.7 0.0 copy-done.1
  71.7 0.0 copy-start.2
  71.7 0.0 copy-start.3
  71.8 1.4 %collective-permute-start.8 = (f32[3,8,2048]{2,1,0:T(8,128)S(1)}, f32[3,8,2048]{2,1,0:T(8,128)S(1)}, u32[]{:S(2)}, u32[]{:S(2)}) collective-permute-start(f32[3,8,2048]{2,1,0:T(8,128)S(1)} %get-tuple-element.19.average), channel_id=1, source_target_pairs={{0,512},{1,513},{2,514},{3,515},{4,516},{5,517},{6,518},{7,519},{8... | collective-permute-start | bytes 589832 | tf_op jit(solution)/shard_map/ppermute | solution.py:478
  73.2 0.0 copy-done.2
  73.2 0.0 copy-done.3
  73.2 1.3 collective-permute-start.9
  74.5 36.0 %collective-permute-done.8.average = f32[3,8,2048]{2,1,0:T(8,128)S(1)} collective-permute-done((f32[3,8,2048]{2,1,0:T(8,128)S(1)}, f32[3,8,2048]{2,1,0:T(8,128)S(1)}, u32[]{:S(2)}, u32[]{:S(2)}) %collective-permute-start.8) | collective-permute-done | bytes 196640 | tf_op jit(solution)/shard_map/ppermute | solution.py:478
  110.6 10.0 %shard_map.82.lower = f32[3,8,2048]{2,1,0:T(8,128)S(1)} custom-call(s32[1]{0:T(128)} %bitcast.flag.refs_0_, f32[3,8,2048]{2,1,0:T(8,128)S(1)} %collective-permute-done.8.average, s32[2,8,2048]{2,1,0:T(8,128)S(1)} %copy-done.2, s32[2,8,2048]{2,1,0:T(8,128)S(1)} %copy-done.3), custom_call_target="tpu_custom_call" | custom-call | tf_op jit(solution)/shard_map/pallas_call | solution.py:469
  120.6 11.3 %collective-permute-done.9.upper = f32[3,8,2048]{2,1,0:T(8,128)S(1)} collective-permute-done((f32[3,8,2048]{2,1,0:T(8,128)S(1)}, f32[3,8,2048]{2,1,0:T(8,128)S(1)}, u32[]{:S(2)}, u32[]{:S(2)}) %collective-permute-start.9) | collective-permute-done | bytes 196640 | tf_op jit(solution)/shard_map/ppermute | solution.py:480
  131.9 0.8 shard_map.84
  (4 shorter events, 0.1 us)
Async XLA Ops:
  0.6 0.9 copy-start
  1.5 1.0 copy-start.4
  2.5 1.0 copy-start.5
  3.5 0.8 copy-start.6
  4.4 32.1 %collective-permute-start = (f32[9,8,2048]{2,1,0:T(8,128)S(1)}, f32[9,8,2048]{2,1,0:T(8,128)S(1)}, u32[]{:S(2)}, u32[]{:S(2)}) collective-permute-start(f32[9,8,2048]{2,1,0:T(8,128)S(1)} %shard_map.77.refs_1_), channel_id=1, source_target_pairs={{0,1},{1,2},{2,3},{3,4},{4,5},{5,6},{6,7},{7,8},{8,9},{9,10},{10,1... | collective-permute-start | bytes 1769480 | tf_op jit(solution)/shard_map/ppermute | solution.py:415
  7.5 29.9 %collective-permute-start.1 = (f32[9,8,2048]{2,1,0:T(8,128)S(1)}, f32[9,8,2048]{2,1,0:T(8,128)S(1)}, u32[]{:S(2)}, u32[]{:S(2)}) collective-permute-start(f32[9,8,2048]{2,1,0:T(8,128)S(1)} %shard_map.77.refs_1_), channel_id=1, source_target_pairs={{1,0},{2,1},{3,2},{4,3},{5,4},{6,5},{7,6},{8,7},{9,8},{10,9},{11,1... | collective-permute-start | bytes 1769480 | tf_op jit(solution)/shard_map/ppermute | solution.py:415
  43.8 1.4 %collective-permute-start.2 = (f32[5,8,2048]{2,1,0:T(8,128)S(1)}, f32[5,8,2048]{2,1,0:T(8,128)S(1)}, u32[]{:S(2)}, u32[]{:S(2)}) collective-permute-start(f32[5,8,2048]{2,1,0:T(8,128)S(1)} %get-tuple-element.11.refs_1_), channel_id=1, source_target_pairs={{0,1},{1,2},{2,3},{3,4},{4,5},{5,6},{6,7},{7,8},{8,9},{9,10},{10,1... | collective-permute-start | bytes 983048 | tf_op jit(solution)/shard_map/ppermute | solution.py:415
  44.5 0.7 collective-permute-start.3
  45.2 15.9 %collective-permute-start.4 = (f32[5,8,2048]{2,1,0:T(8,128)S(1)}, f32[5,8,2048]{2,1,0:T(8,128)S(1)}, u32[]{:S(2)}, u32[]{:S(2)}) collective-permute-start(f32[5,8,2048]{2,1,0:T(8,128)S(1)} %get-tuple-element.14.refs_1_), channel_id=1, source_target_pairs={{0,1},{1,2},{2,3},{3,4},{4,5},{5,6},{6,7},{7,8},{8,9},{9,10},{10,1... | collective-permute-start | bytes 983048 | tf_op jit(solution)/shard_map/ppermute | solution.py:415
  47.2 15.8 %collective-permute-start.5 = (f32[5,8,2048]{2,1,0:T(8,128)S(1)}, f32[5,8,2048]{2,1,0:T(8,128)S(1)}, u32[]{:S(2)}, u32[]{:S(2)}) collective-permute-start(f32[5,8,2048]{2,1,0:T(8,128)S(1)} %get-tuple-element.14.refs_1_), channel_id=1, source_target_pairs={{1,0},{2,1},{3,2},{4,3},{5,4},{6,5},{7,6},{8,7},{9,8},{10,9},{11,1... | collective-permute-start | bytes 983048 | tf_op jit(solution)/shard_map/ppermute | solution.py:415
  62.9 8.7 %copy-start.7 = (s32[8,2048]{1,0:T(8,128)S(1)}, s32[8,2048]{1,0:T(8,128)}, u32[]{:S(2)}) copy-start(s32[8,2048]{1,0:T(8,128)} %refs_8_.1) | copy-start | bytes 196612
  69.3 2.4 %copy-start.1 = (f32[2,8,2048]{2,1,0:T(8,128)S(1)}, f32[2,8,2048]{2,1,0:T(8,128)}, u32[]{:S(2)}) copy-start(f32[2,8,2048]{2,1,0:T(8,128)} %refs_7_.1) | copy-start | bytes 393220
  69.3 2.4 %collective-permute-start.6 = (f32[5,8,2048]{2,1,0:T(8,128)S(1)}, f32[5,8,2048]{2,1,0:T(8,128)S(1)}, u32[]{:S(2)}, u32[]{:S(2)}) collective-permute-start(f32[5,8,2048]{2,1,0:T(8,128)S(1)} %get-tuple-element.16.refs_1_), channel_id=1, source_target_pairs={{0,1},{1,2},{2,3},{3,4},{4,5},{5,6},{6,7},{7,8},{8,9},{9,10},{10,1... | collective-permute-start | bytes 983048 | tf_op jit(solution)/shard_map/ppermute | solution.py:415
  70.1 1.5 %collective-permute-start.7 = (f32[5,8,2048]{2,1,0:T(8,128)S(1)}, f32[5,8,2048]{2,1,0:T(8,128)S(1)}, u32[]{:S(2)}, u32[]{:S(2)}) collective-permute-start(f32[5,8,2048]{2,1,0:T(8,128)S(1)} %get-tuple-element.16.refs_1_), channel_id=1, source_target_pairs={{1,0},{2,1},{3,2},{4,3},{5,4},{6,5},{7,6},{8,7},{9,8},{10,9},{11,1... | collective-permute-start | bytes 983048 | tf_op jit(solution)/shard_map/ppermute | solution.py:415
  71.7 1.5 %copy-start.2 = (s32[2,8,2048]{2,1,0:T(8,128)S(1)}, s32[2,8,2048]{2,1,0:T(8,128)}, u32[]{:S(2)}) copy-start(s32[2,8,2048]{2,1,0:T(8,128)} %targets.3) | copy-start | bytes 393220
  71.7 1.5 %copy-start.3 = (s32[2,8,2048]{2,1,0:T(8,128)S(1)}, s32[2,8,2048]{2,1,0:T(8,128)}, u32[]{:S(2)}) copy-start(s32[2,8,2048]{2,1,0:T(8,128)} %weights.3) | copy-start | bytes 393220
  71.8 38.8 %collective-permute-start.8 = (f32[3,8,2048]{2,1,0:T(8,128)S(1)}, f32[3,8,2048]{2,1,0:T(8,128)S(1)}, u32[]{:S(2)}, u32[]{:S(2)}) collective-permute-start(f32[3,8,2048]{2,1,0:T(8,128)S(1)} %get-tuple-element.19.average), channel_id=1, source_target_pairs={{0,512},{1,513},{2,514},{3,515},{4,516},{5,517},{6,518},{7,519},{8... | collective-permute-start | bytes 589832 | tf_op jit(solution)/shard_map/ppermute | solution.py:478
  73.2 58.6 %collective-permute-start.9 = (f32[3,8,2048]{2,1,0:T(8,128)S(1)}, f32[3,8,2048]{2,1,0:T(8,128)S(1)}, u32[]{:S(2)}, u32[]{:S(2)}) collective-permute-start(f32[3,8,2048]{2,1,0:T(8,128)S(1)} %shard_map.83), channel_id=1, source_target_pairs={{0,513},{1,514},{2,515},{3,516},{4,517},{5,518},{6,519},{7,520},{8... | collective-permute-start | bytes 589832 | tf_op jit(solution)/shard_map/ppermute | solution.py:480

commit v2 on v1

--- a/solution.py
+++ b/solution.py
@@ -1,3 +1,5 @@
+from functools import partial
+
 import jax
 import jax.numpy as jnp
 from jax import lax
@@ -10,7 +12,8 @@
 OCEAN_DEPTH = 8
 LANES = 128
 PAD = 8
-GROUP = 4
+GROUP = 16
+OCEAN_DELAY = 12000
 
 keep = 1.0 / 1.5
 gain = 0.5 / 1.5
@@ -27,8 +30,18 @@
 LIMITED = pltpu.CompilerParams(vmem_limit_bytes=20 * 1024 * 1024)
 
 
-def prep_kernel(flag, initial, forcing, current, cover, out):
-    @pl.when(flag[0] == 0)
+def prep_kernel(strips, flag, *refs):
+    sources, out, (initial, forcing, current, cover), arrived = refs[:4], refs[4], refs[5:9], refs[9]
+    copies = [
+        pltpu.make_async_copy(source, target, arrived.at[i])
+        for i, (source, target) in enumerate(zip(sources, (initial, forcing, current, cover)))
+    ]
+    for copy in copies:
+        copy.start()
+    for copy in copies:
+        copy.wait()
+
+    @pl.when(flag[0] < strips)
     def _():
         out[0] = initial[0, 0]
         out[1] = initial[0, 1]
@@ -42,8 +55,9 @@
         out[7] = g * (forcing[2] + drag_coef * current[0])
         out[8] = g * (forcing[3] + drag_coef * current[1])
 
-    @pl.when(flag[0] != 0)
+    @pl.when(flag[0] >= strips)
     def _():
+        pl.delay(OCEAN_DELAY)
         for level in range(5):
             out[level] = initial[0, level]
         out[5] = current[0]
@@ -52,16 +66,15 @@
         out[8] = jnp.zeros_like(current[0])
 
 
-def load_window(dst, dst_plane, src_plane, low, own, high, tiles, base):
-    rows = own.shape[1]
-    for part, ref in enumerate((low, own, high)):
-        for c in range(tiles):
-            dst[dst_plane, base[1] + c, pl.ds(base[0] + part * rows, rows), :] = ref[
-                src_plane, :, c * LANES : (c + 1) * LANES
-            ]
-
-
-def make_round(first, last, ocean_active, rows, tiles):
+def load_strip(dst, dst_plane, src, src_plane, part, tiles, base):
+    rows = src.shape[1]
+    for c in range(tiles):
+        dst[dst_plane, base[1] + c, pl.ds(base[0] + part * rows, rows), :] = src[
+            src_plane, :, c * LANES : (c + 1) * LANES
+        ]
+
+
+def make_round(strips, first, last, ocean_active, rows, tiles):
     window = 3 * rows
     low_off = PAD
 
@@ -76,17 +89,19 @@
     def kernel(*refs):
         refs = list(refs)
         flag = refs.pop(0)
-        own, low, high = refs[:3]
+        own, near, far = refs[:3]
         refs = refs[3:]
-        if not first:
+        if first:
+            targets, weights = refs[:2]
+        else:
             stat, total_in = refs[:2]
-            refs = refs[2:]
+        refs = refs[2:]
         if last:
             melt, current, cover = refs[:3]
             refs = refs[3:]
         if first:
-            out, total, stat = refs[:3]
-            refs = refs[3:]
+            out, total, stat, links = refs[:4]
+            refs = refs[4:]
         else:
             out, total = refs[:2]
             refs = refs[2:]
@@ -95,6 +110,19 @@
         lane = lax.broadcasted_iota(jnp.int32, (8, LANES), 1)
         at_first = lane == 0
         at_last = lane == LANES - 1
+        odd = jnp.bitwise_and(flag[0], 1) == 1
+
+        def load_windows(dst, planes, base):
+            def halo(low, high):
+                for plane, source in planes:
+                    load_strip(dst, plane, low, source, 0, tiles, base)
+                    load_strip(dst, plane, high, source, 2, tiles, base)
+
+            for plane, source in planes:
+                load_strip(dst, plane, own, source, 1, tiles, base)
+            pl.when(odd)(lambda: halo(near, far))
+            pl.when(jnp.logical_not(odd))(lambda: halo(far, near))
+
         zero_column = jnp.zeros((window + 2 * PAD, LANES), jnp.float32)
 
         def sides(ref, plane, column, row, cache):
@@ -122,15 +150,14 @@
 
         def ice():
             if first:
-                for plane in range(4):
-                    load_window(stat, plane, 5 + plane, low, own, high, tiles, (0, 0))
+                load_windows(stat, [(plane, 5 + plane) for plane in range(4)], (0, 0))
                 for part in range(3):
                     total[part] = jnp.zeros((rows, tiles * LANES), jnp.float32)
             else:
                 for part in range(3):
                     total[part] = total_in[part]
+            load_windows(field, [(plane, plane) for plane in range(5)], (low_off, 1))
             for plane in range(5):
-                load_window(field, plane, plane, low, own, high, tiles, (low_off, 1))
                 field[plane, 0] = zero_column
                 field[plane, tiles + 1] = zero_column
 
@@ -252,13 +279,15 @@
 
         def ocean():
             if first:
-                for plane in range(2):
-                    load_window(stat, plane, 5 + plane, low, own, high, tiles, (0, 0))
+                load_windows(stat, [(plane, 5 + plane) for plane in range(2)], (0, 0))
+                for entry in range(2):
+                    links[entry] = targets[entry].astype(jnp.float32)
+                    links[2 + entry] = weights[entry].astype(jnp.float32)
             if not ocean_active:
                 out[...] = own[:5]
                 return
+            load_windows(field, [(plane, plane) for plane in range(5)], (low_off, 1))
             for plane in range(5):
-                load_window(field, plane, plane, low, own, high, tiles, (low_off, 1))
                 for ref in (field, other):
                     ref[plane, 0] = zero_column
                     ref[plane, tiles + 1] = zero_column
@@ -306,37 +335,37 @@
                         p, c + 1, low_off + rows : low_off + 2 * rows, :
                     ]
 
-        @pl.when(flag[0] == 0)
+        @pl.when(flag[0] < strips)
         def _():
             ice()
 
-        @pl.when(flag[0] != 0)
+        @pl.when(flag[0] >= strips)
         def _():
             ocean()
 
     return kernel
 
 
-HIGH = 64
 WIDE = 256
 
 
-def scatter_half(half, values, targets, weights, out, left, right, sums):
+def scatter_half(half, values, spots_of, weights_of, sums, blocks):
     rows = values.shape[1]
     columns = values.shape[2]
     groups = columns // WIDE
     spots = rows * groups
+    turns = 2 * rows
     sums[...] = jnp.zeros_like(sums)
     high_at = lax.broadcasted_iota(jnp.int32, (spots, columns), 0).astype(jnp.bfloat16)
     low_at = lax.broadcasted_iota(jnp.int32, (WIDE, columns), 0).astype(jnp.bfloat16)
     zero = jnp.zeros((), jnp.bfloat16)
     one = jnp.ones((), jnp.bfloat16)
 
-    def step(turn, carry):
+    def build(turn, left, right):
         entry = turn // rows
         row = turn % rows
-        spot = targets[entry, pl.ds(row, 1), :]
-        scale = weights[entry, pl.ds(row, 1), :].astype(jnp.float32) / weight_norm
+        spot = spots_of[entry, pl.ds(row, 1), :].astype(jnp.int32)
+        scale = weights_of[entry, pl.ds(row, 1), :].astype(jnp.float32) / weight_norm
         low = jnp.bitwise_and(spot, WIDE - 1)
         high = jnp.right_shift(spot, 8) - half * spots
         inside = jnp.logical_and(high >= 0, high < spots)
@@ -350,47 +379,63 @@
             value = values[channel, pl.ds(row, 1), :] * scale
             coarse = value.astype(jnp.bfloat16)
             fine = (value - coarse.astype(jnp.float32)).astype(jnp.bfloat16)
-            left[2 * channel * spots : (2 * channel + 1) * spots, :] = jnp.where(hit, coarse, zero)
-            left[(2 * channel + 1) * spots : (2 * channel + 2) * spots, :] = jnp.where(
-                hit, fine, zero
-            )
+            for part, piece in enumerate((coarse, fine)):
+                first = (2 * channel + part) * spots
+                left[first : first + spots, :] = jnp.where(hit, piece, zero)
+
+    def multiply(left, right):
         sums[...] += lax.dot_general(
             left[...],
             right[...],
             (((1,), (1,)), ((), ())),
             preferred_element_type=jnp.float32,
         )
+
+    left_a, right_a, left_b, right_b = blocks
+    build(0, left_a, right_a)
+
+    def step(pair, carry):
+        build(2 * pair + 1, left_b, right_b)
+        multiply(left_a, right_a)
+        build(jnp.minimum(2 * pair + 2, turns - 1), left_a, right_a)
+        multiply(left_b, right_b)
         return carry
 
-    lax.fori_loop(0, 2 * rows, step, 0)
+    lax.fori_loop(0, turns // 2, step, 0)
+
+    def tile(channel, group):
+        first = 2 * channel * spots + group * rows
+        return sums[first : first + rows, :] + sums[first + spots : first + spots + rows, :]
+
+    return tile, groups
+
+
+def write_half(half, values, spots_of, weights_of, out, sums, blocks):
+    tile, groups = scatter_half(half, values, spots_of, weights_of, sums, blocks)
     for channel in range(3):
         for g in range(groups):
-            first = 2 * channel * spots + g * rows
-            second = first + spots
-            out[channel, :, g * WIDE : (g + 1) * WIDE] = (
-                sums[first : first + rows, :] + sums[second : second + rows, :]
-            )
-
-
-def upper_kernel(flag, average, targets, weights, out, left, right, sums):
-    @pl.when(flag[0] == 0)
+            out[channel, :, g * WIDE : (g + 1) * WIDE] = tile(channel, g)
+
+
+def lower_kernel(strips, flag, average, targets, weights, out, sums, *blocks):
+    @pl.when(flag[0] < strips)
     def _():
-        scatter_half(1, average, targets, weights, out, left, right, sums)
-
-
-def lower_kernel(flag, average, targets, weights, out, left, right, sums):
-    @pl.when(flag[0] != 0)
+        write_half(0, average, targets, weights, out, sums, blocks)
+
+
+def upper_kernel(strips, flag, before, links, out, sums, *blocks):
+    @pl.when(flag[0] >= strips)
     def _():
-        scatter_half(0, average, targets, weights, out, left, right, sums)
-
-
-def final_kernel(flag, fields, average, lower, upper, state, coupled):
-    @pl.when(flag[0] == 0)
+        write_half(1, before, links.at[:2], links.at[2:], out, sums, blocks)
+
+
+def final_kernel(strips, flag, fields, average, lower, upper, state, coupled):
+    @pl.when(flag[0] < strips)
     def _():
         state[0] = fields[...]
         coupled[0] = average[...]
 
-    @pl.when(flag[0] != 0)
+    @pl.when(flag[0] >= strips)
     def _():
         flux = lower[...] + upper[...]
         coupled[0] = flux
@@ -402,15 +447,15 @@
     rows, columns = initial.shape[2:]
     tiles = columns // LANES
     strips = lax.axis_size("blk")
-    flag = lax.axis_index("comp").astype(jnp.int32).reshape(1)
     both = ("comp", "blk")
-
-    def moved(value, kinds, step):
+    flag = lax.axis_index(both).astype(jnp.int32).reshape(1)
+
+    def swapped(value, kinds, start):
         pairs = [
-            (kind * strips + b, kind * strips + b + step)
+            (kind * strips + source, kind * strips + target)
             for kind in kinds
-            for b in range(strips)
-            if 0 <= b + step < strips
+            for b in range(start, strips - 1, 2)
+            for source, target in ((b, b + 1), (b + 1, b))
         ]
         return lax.ppermute(value, both, pairs)
 
@@ -421,12 +466,23 @@
         return [pltpu.with_memory_space_constraint(value, pltpu.VMEM) for value in values]
 
     block = pl.pallas_call(
-        prep_kernel,
+        partial(prep_kernel, strips),
         compiler_params=LIMITED,
         out_shape=shape(9, rows, columns),
-        in_specs=[SMEM] + [VMEM] * 4,
+        in_specs=[SMEM] + [pl.BlockSpec(memory_space=pltpu.HBM)] * 4,
         out_specs=VMEM,
-    )(flag, initial, ice_forcing, ocean_current, ice_cover)
+        scratch_shapes=[
+            pltpu.VMEM(value.shape, value.dtype)
+            for value in (initial, ice_forcing, ocean_current, ice_cover)
+        ]
+        + [pltpu.SemaphoreType.DMA((4,))],
+    )(
+        flag,
+        *(
+            pltpu.with_memory_space_constraint(value, pltpu.HBM)
+            for value in (initial, ice_forcing, ocean_current, ice_cover)
+        ),
+    )
 
     rounds = SUBCYCLES // ICE_DEPTH
     each = OCEAN_DEPTH // ICE_DEPTH
@@ -436,18 +492,17 @@
         first, last = turn == 0, turn == rounds - 1
         active = turn % each == 0
         kinds = (0, 1) if active else (0,)
-        low = moved(block, kinds, 1)
-        high = moved(block, kinds, -1)
-        operands = [flag, block, low, high]
+        near = swapped(block, kinds, 0)
+        far = swapped(block, kinds, 1)
+        operands = [flag, block, near, far]
         outs = [shape(5, rows, columns), shape(3, rows, columns)]
-        if not first:
-            operands += [stat, total]
+        operands += [targets, weights] if first else [stat, total]
         if last:
             operands += [ice_forcing[4:], ocean_current, ice_cover]
         if first:
-            outs.append(shape(4, tiles, window, LANES))
+            outs += [shape(4, tiles, window, LANES), shape(4, rows, columns)]
         done = pl.pallas_call(
-            make_round(first, last, active, rows, tiles),
+            make_round(strips, first, last, active, rows, tiles),
             compiler_params=LIMITED,
             out_shape=outs,
             in_specs=[SMEM] + [VMEM] * (len(operands) - 1),
@@ -456,32 +511,35 @@
         )(flag, *held(*operands[1:]))
         block, total = done[:2]
         if first:
-            stat = done[2]
+            stat, links = done[2:]
 
     average = total
-    scatter_scratch = [
-        pltpu.VMEM((6 * rows * columns // WIDE, columns), jnp.bfloat16),
+    links_before = lax.ppermute(
+        links, both, [(strips + b, strips + (b + 1) % strips) for b in range(strips)]
+    )
+    before = lax.ppermute(average, both, [(b, strips + (b + 1) % strips) for b in range(strips)])
+    spots = rows * columns // WIDE
+    scratch = [pltpu.VMEM((6 * spots, WIDE), jnp.float32)] + [
+        pltpu.VMEM((6 * spots, columns), jnp.bfloat16),
         pltpu.VMEM((WIDE, columns), jnp.bfloat16),
-        pltpu.VMEM((6 * rows * columns // WIDE, WIDE), jnp.float32),
-    ]
-
-    def scattered(kernel, values):
+    ] * 2
+
+    def scattered(kernel, *operands):
         return pl.pallas_call(
-            kernel,
+            partial(kernel, strips),
             compiler_params=LIMITED,
             out_shape=shape(3, rows, columns),
-            in_specs=[SMEM] + [VMEM] * 3,
+            in_specs=[SMEM] + [VMEM] * len(operands),
             out_specs=VMEM,
-            scratch_shapes=scatter_scratch,
-        )(flag, *held(values, targets, weights))
-
-    received = lax.ppermute(average, both, [(b, strips + b) for b in range(strips)])
-    upper = scattered(upper_kernel, average)
-    beyond = lax.ppermute(upper, both, [(b, strips + (b + 1) % strips) for b in range(strips)])
-    lower = scattered(lower_kernel, received)
+            scratch_shapes=scratch,
+        )(flag, *held(*operands))
+
+    lower = scattered(lower_kernel, average, targets, weights)
+    received = lax.ppermute(lower, both, [(b, strips + b) for b in range(strips)])
+    upper = scattered(upper_kernel, before, links_before)
     return tuple(
         pl.pallas_call(
-            final_kernel,
+            partial(final_kernel, strips),
             compiler_params=LIMITED,
             out_shape=[
                 jax.ShapeDtypeStruct((1, 5, rows, columns), jnp.float32),
@@ -489,7 +547,7 @@
             ],
             in_specs=[SMEM] + [VMEM] * 4,
             out_specs=[VMEM] * 2,
-        )(flag, *held(block, average, lower, beyond))
+        )(flag, *held(block, average, received, upper))
     )
 
 

time: 133 us -> 111 us (0.83)
  waiting for transfers between devices: 65.5 us -> 38.3 us
  Pallas kernels: 23.7 us -> 30.6 us
  local copies, waits for them, and re-layouts: 4.55 us -> 0.87 us
  starting transfers between devices: 38.1 us -> 40.3 us
    ppermute x10 -> x11, waiting for transfers between devices: 65.5 us -> 38.3 us  [the longest x1 19.5 us: body(): lax.ppermute(average, both, [(b, strips + (b + 1) % strips) for b in rang...]
    pallas_call x8, Pallas kernels: 23.7 us -> 30.6 us  [the longest x1 13.2 us: body(): pl.pallas_call(partial(prep_kernel, strips), compiler_params=LIMITED, out...]
    unnamed x16 -> x8, local copies, waits for them, and re-layouts: 3.71 us -> 0.02 us
    ppermute x10 -> x11, starting transfers between devices: 38.1 us -> 40.3 us  [the longest x8 35.8 us: swapped(): return lax.ppermute(value, both, pairs)]
  transfers between devices with their start and end apart: 10 -> 11, of which waited for: 6 -> 4; matrix products, arithmetic and copies ran while one was open for 1% -> 1% of each run, Pallas kernels for 8% -> 8%
where the time goes in v2:
time: 111 us
  starting transfers between devices  40.3 us (36%)
  waiting for transfers between devices  38.3 us (35%)
  Pallas kernels  30.6 us (28%)
    ppermute x8, starting transfers between devices, swapped(): return lax.ppermute(value, both, pairs)  35.8 us
    ppermute x1, waiting for transfers between devices, body(): lax.ppermute(average, both, [(b, strips + (b + 1) % strips) for b in rang...  19.5 us
    pallas_call x1, Pallas kernels, body(): pl.pallas_call(partial(prep_kernel, strips), compiler_params=LIMITED, out...  13.2 us
    ppermute x8, waiting for transfers between devices, swapped(): return lax.ppermute(value, both, pairs)  11.7 us
    pallas_call x2, Pallas kernels, scattered(): pl.pallas_call(partial(kernel, strips), compiler_params=LIMITED, out_shap...  8.8 us
    pallas_call x4, Pallas kernels, body(): pl.pallas_call(make_round(strips, first, last, active, rows, tiles), comp...  7.69 us
    ppermute x1, waiting for transfers between devices, body(): lax.ppermute(links, both, [(strips + b, strips + (b + 1) % strips) for b...  7.08 us
  transfers between devices with their start and end apart: 11, of which 4 were waited for; matrix products, arithmetic and copies ran while one was open for 1% of the time, Pallas kernels for 8%

profile of v2, /device:TPU:65, one launch (start us, length us, event | category | flops | bytes accessed | tf_op | source)
XLA Modules:
  0.0 110.8 jit_solution(786528700575644583)
XLA Ops:
  0.6 0.0 copy-start
  0.6 0.0 copy-start.1
  0.7 13.2 %shard_map.77.refs_1_ = f32[9,8,2048]{2,1,0:T(8,128)S(1)} custom-call(s32[1]{0:T(128)} %bitcast.flag.refs_0_, f32[1,5,8,2048]{3,2,1,0:T(8,128)} %refs_0_.1, f32[5,8,2048]{2,1,0:T(8,128)} %refs_1_.1, f32[2,8,2048]{2,1,0:T(8,128)} %refs_7_.1, s32[8,2048]{1,0:T(8,128)} %refs_8_.1), custom_call_target="tpu_custom_call" | custom-call | tf_op jit(solution)/shard_map/pallas_call | solution.py:468
  13.9 3.1 %collective-permute-start = (f32[9,8,2048]{2,1,0:T(8,128)S(1)}, f32[9,8,2048]{2,1,0:T(8,128)S(1)}, u32[]{:S(2)}, u32[]{:S(2)}) collective-permute-start(f32[9,8,2048]{2,1,0:T(8,128)S(1)} %shard_map.77.refs_1_), channel_id=1, source_target_pairs={{0,1},{1,0},{2,3},{3,2},{4,5},{5,4},{6,7},{7,6},{8,9},{9,8},{10,11... | collective-permute-start | bytes 1769480 | tf_op jit(solution)/shard_map/ppermute | solution.py:460
  17.0 19.1 %collective-permute-start.1 = (f32[9,8,2048]{2,1,0:T(8,128)S(1)}, f32[9,8,2048]{2,1,0:T(8,128)S(1)}, u32[]{:S(2)}, u32[]{:S(2)}) collective-permute-start(f32[9,8,2048]{2,1,0:T(8,128)S(1)} %shard_map.77.refs_1_), channel_id=1, source_target_pairs={{1,2},{2,1},{3,4},{4,3},{5,6},{6,5},{7,8},{8,7},{9,10},{10,9},{11,... | collective-permute-start | bytes 1769480 | tf_op jit(solution)/shard_map/ppermute | solution.py:460
  36.1 0.0 collective-permute-done.refs_2_
  36.1 7.2 %collective-permute-done.1.refs_3_ = f32[9,8,2048]{2,1,0:T(8,128)S(1)} collective-permute-done((f32[9,8,2048]{2,1,0:T(8,128)S(1)}, f32[9,8,2048]{2,1,0:T(8,128)S(1)}, u32[]{:S(2)}, u32[]{:S(2)}) %collective-permute-start.1) | collective-permute-done | bytes 589856 | tf_op jit(solution)/shard_map/ppermute | solution.py:460
  43.3 0.0 copy-done
  43.3 0.0 copy-done.1
  43.3 3.6 %shard_map.78 = (f32[5,8,2048]{2,1,0:T(8,128)S(1)}, f32[3,8,2048]{2,1,0:T(8,128)S(1)}, f32[4,16,24,128]{3,2,1,0:T(8,128)S(1)}, f32[4,8,2048]{2,1,0:T(8,128)S(1)}) custom-call(s32[1]{0:T(128)} %bitcast.flag.refs_0_, f32[9,8,2048]{2,1,0:T(8,128)S(1)} %shard_map.77.refs_1_, f32[9,8,2048]{2,1,0:T(8,128)S(1)} %collective-permute-done.refs_2_, ...), custom_call_target="tpu_custom_call" | custom-call | tf_op jit(solution)/shard_map/pallas_call | solution.py:504
  47.0 0.7 collective-permute-start.2
  47.7 0.7 collective-permute-start.3
  48.4 0.0 collective-permute-done.2.refs_2_
  48.4 0.0 collective-permute-done.3.refs_3_
  48.4 1.9 %collective-permute-start.4 = (f32[5,8,2048]{2,1,0:T(8,128)S(1)}, f32[5,8,2048]{2,1,0:T(8,128)S(1)}, u32[]{:S(2)}, u32[]{:S(2)}) collective-permute-start(f32[5,8,2048]{2,1,0:T(8,128)S(1)} %get-tuple-element.15.refs_1_), channel_id=1, source_target_pairs={{0,1},{1,0},{2,3},{3,2},{4,5},{5,4},{6,7},{7,6},{8,9},{9,8},{10,11... | collective-permute-start | bytes 983048 | tf_op jit(solution)/shard_map/ppermute | solution.py:460
  50.4 8.8 %collective-permute-start.5 = (f32[5,8,2048]{2,1,0:T(8,128)S(1)}, f32[5,8,2048]{2,1,0:T(8,128)S(1)}, u32[]{:S(2)}, u32[]{:S(2)}) collective-permute-start(f32[5,8,2048]{2,1,0:T(8,128)S(1)} %get-tuple-element.15.refs_1_), channel_id=1, source_target_pairs={{1,2},{2,1},{3,4},{4,3},{5,6},{6,5},{7,8},{8,7},{9,10},{10,9},{11,... | collective-permute-start | bytes 983048 | tf_op jit(solution)/shard_map/ppermute | solution.py:460
  59.2 0.0 collective-permute-done.4.refs_2_
  59.2 4.4 %collective-permute-done.5.refs_3_ = f32[5,8,2048]{2,1,0:T(8,128)S(1)} collective-permute-done((f32[5,8,2048]{2,1,0:T(8,128)S(1)}, f32[5,8,2048]{2,1,0:T(8,128)S(1)}, u32[]{:S(2)}, u32[]{:S(2)}) %collective-permute-start.5) | collective-permute-done | bytes 327712 | tf_op jit(solution)/shard_map/ppermute | solution.py:460
  63.6 0.0 copy-start.3
  63.6 4.0 %shard_map.80 = (f32[5,8,2048]{2,1,0:T(8,128)S(1)}, f32[3,8,2048]{2,1,0:T(8,128)S(1)}) custom-call(s32[1]{0:T(128)} %bitcast.flag.refs_0_, f32[5,8,2048]{2,1,0:T(8,128)S(1)} %get-tuple-element.15.refs_1_, f32[5,8,2048]{2,1,0:T(8,128)S(1)} %collective-permute-done.4.refs_2_, f32[5,8,2048]{2,1,0:T(8,128)S(1)} %collective-permute-done.5.refs_3_, ...), custom_call_target="tpu_custom_call" | custom-call | tf_op jit(solution)/shard_map/pallas_call | solution.py:504
  67.6 0.0 copy-start.2
  67.6 0.8 collective-permute-start.6
  68.4 0.7 collective-permute-start.7
  69.1 1.9 %collective-permute-start.10 = (f32[4,8,2048]{2,1,0:T(8,128)S(1)}, f32[4,8,2048]{2,1,0:T(8,128)S(1)}, u32[]{:S(2)}, u32[]{:S(2)}) collective-permute-start(f32[4,8,2048]{2,1,0:T(8,128)S(1)} %get-tuple-element.21), channel_id=1, source_target_pairs={{512,513},{513,514},{514,515},{515,516},{516,517},{517,518},{518,5... | collective-permute-start | bytes 786440 | tf_op jit(solution)/shard_map/ppermute | solution.py:517
  71.1 0.8 slice.3.refs_6_
  71.9 0.0 collective-permute-done.6.refs_2_
  71.9 0.0 collective-permute-done.7.refs_3_
  71.9 0.0 copy-done.3
  71.9 0.0 copy-done.2
  72.0 1.3 %collective-permute-start.9 = (f32[3,8,2048]{2,1,0:T(8,128)S(1)}, f32[3,8,2048]{2,1,0:T(8,128)S(1)}, u32[]{:S(2)}, u32[]{:S(2)}) collective-permute-start(f32[3,8,2048]{2,1,0:T(8,128)S(1)} %get-tuple-element.20.average), channel_id=1, source_target_pairs={{0,513},{1,514},{2,515},{3,516},{4,517},{5,518},{6,519},{7,520},{8... | collective-permute-start | bytes 589832 | tf_op jit(solution)/shard_map/ppermute | solution.py:520
  73.3 1.3 %collective-permute-start.8 = (f32[3,8,2048]{2,1,0:T(8,128)S(1)}, f32[3,8,2048]{2,1,0:T(8,128)S(1)}, u32[]{:S(2)}, u32[]{:S(2)}) collective-permute-start(f32[3,8,2048]{2,1,0:T(8,128)S(1)} %shard_map.82), channel_id=1, source_target_pairs={{0,512},{1,513},{2,514},{3,515},{4,516},{5,517},{6,518},{7,519},{8... | collective-permute-start | bytes 589832 | tf_op jit(solution)/shard_map/ppermute | solution.py:538
  74.6 7.1 %collective-permute-done.10.links = f32[4,8,2048]{2,1,0:T(8,128)S(1)} collective-permute-done((f32[4,8,2048]{2,1,0:T(8,128)S(1)}, f32[4,8,2048]{2,1,0:T(8,128)S(1)}, u32[]{:S(2)}, u32[]{:S(2)}) %collective-permute-start.10) | collective-permute-done | bytes 262176 | tf_op jit(solution)/shard_map/ppermute | solution.py:517
  81.7 19.5 %collective-permute-done.9.before = f32[3,8,2048]{2,1,0:T(8,128)S(1)} collective-permute-done((f32[3,8,2048]{2,1,0:T(8,128)S(1)}, f32[3,8,2048]{2,1,0:T(8,128)S(1)}, u32[]{:S(2)}, u32[]{:S(2)}) %collective-permute-start.9) | collective-permute-done | bytes 196640 | tf_op jit(solution)/shard_map/ppermute | solution.py:520
  101.2 8.8 %shard_map.83.upper = f32[3,8,2048]{2,1,0:T(8,128)S(1)} custom-call(s32[1]{0:T(128)} %bitcast.flag.refs_0_, f32[3,8,2048]{2,1,0:T(8,128)S(1)} %collective-permute-done.9.before, f32[4,8,2048]{2,1,0:T(8,128)S(1)} %collective-permute-done.10.links), custom_call_target="tpu_custom_call" | custom-call | tf_op jit(solution)/shard_map/pallas_call | solution.py:528
  110.0 0.0 collective-permute-done.8.lower
  110.0 0.8 shard_map.84
  (3 shorter events, 0.1 us)
Async XLA Ops:
  0.6 42.7 %copy-start = (s32[2,8,2048]{2,1,0:T(8,128)S(1)}, s32[2,8,2048]{2,1,0:T(8,128)}, u32[]{:S(2)}) copy-start(s32[2,8,2048]{2,1,0:T(8,128)} %targets.1) | copy-start | bytes 393220
  0.6 42.7 %copy-start.1 = (s32[2,8,2048]{2,1,0:T(8,128)S(1)}, s32[2,8,2048]{2,1,0:T(8,128)}, u32[]{:S(2)}) copy-start(s32[2,8,2048]{2,1,0:T(8,128)} %weights.1) | copy-start | bytes 393220
  13.9 22.2 %collective-permute-start = (f32[9,8,2048]{2,1,0:T(8,128)S(1)}, f32[9,8,2048]{2,1,0:T(8,128)S(1)}, u32[]{:S(2)}, u32[]{:S(2)}) collective-permute-start(f32[9,8,2048]{2,1,0:T(8,128)S(1)} %shard_map.77.refs_1_), channel_id=1, source_target_pairs={{0,1},{1,0},{2,3},{3,2},{4,5},{5,4},{6,7},{7,6},{8,9},{9,8},{10,11... | collective-permute-start | bytes 1769480 | tf_op jit(solution)/shard_map/ppermute | solution.py:460
  17.0 26.3 %collective-permute-start.1 = (f32[9,8,2048]{2,1,0:T(8,128)S(1)}, f32[9,8,2048]{2,1,0:T(8,128)S(1)}, u32[]{:S(2)}, u32[]{:S(2)}) collective-permute-start(f32[9,8,2048]{2,1,0:T(8,128)S(1)} %shard_map.77.refs_1_), channel_id=1, source_target_pairs={{1,2},{2,1},{3,4},{4,3},{5,6},{6,5},{7,8},{8,7},{9,10},{10,9},{11,... | collective-permute-start | bytes 1769480 | tf_op jit(solution)/shard_map/ppermute | solution.py:460
  47.0 1.4 %collective-permute-start.2 = (f32[5,8,2048]{2,1,0:T(8,128)S(1)}, f32[5,8,2048]{2,1,0:T(8,128)S(1)}, u32[]{:S(2)}, u32[]{:S(2)}) collective-permute-start(f32[5,8,2048]{2,1,0:T(8,128)S(1)} %get-tuple-element.12.refs_1_), channel_id=1, source_target_pairs={{0,1},{1,0},{2,3},{3,2},{4,5},{5,4},{6,7},{7,6},{8,9},{9,8},{10,11... | collective-permute-start | bytes 983048 | tf_op jit(solution)/shard_map/ppermute | solution.py:460
  47.7 0.7 collective-permute-start.3
  48.4 10.7 %collective-permute-start.4 = (f32[5,8,2048]{2,1,0:T(8,128)S(1)}, f32[5,8,2048]{2,1,0:T(8,128)S(1)}, u32[]{:S(2)}, u32[]{:S(2)}) collective-permute-start(f32[5,8,2048]{2,1,0:T(8,128)S(1)} %get-tuple-element.15.refs_1_), channel_id=1, source_target_pairs={{0,1},{1,0},{2,3},{3,2},{4,5},{5,4},{6,7},{7,6},{8,9},{9,8},{10,11... | collective-permute-start | bytes 983048 | tf_op jit(solution)/shard_map/ppermute | solution.py:460
  50.4 13.3 %collective-permute-start.5 = (f32[5,8,2048]{2,1,0:T(8,128)S(1)}, f32[5,8,2048]{2,1,0:T(8,128)S(1)}, u32[]{:S(2)}, u32[]{:S(2)}) collective-permute-start(f32[5,8,2048]{2,1,0:T(8,128)S(1)} %get-tuple-element.15.refs_1_), channel_id=1, source_target_pairs={{1,2},{2,1},{3,4},{4,3},{5,6},{6,5},{7,8},{8,7},{9,10},{10,9},{11,... | collective-permute-start | bytes 983048 | tf_op jit(solution)/shard_map/ppermute | solution.py:460
  63.6 8.3 %copy-start.3 = (s32[8,2048]{1,0:T(8,128)S(1)}, s32[8,2048]{1,0:T(8,128)}, u32[]{:S(2)}) copy-start(s32[8,2048]{1,0:T(8,128)} %refs_8_.1) | copy-start | bytes 196612
  67.6 4.3 %copy-start.2 = (f32[2,8,2048]{2,1,0:T(8,128)S(1)}, f32[2,8,2048]{2,1,0:T(8,128)}, u32[]{:S(2)}) copy-start(f32[2,8,2048]{2,1,0:T(8,128)} %refs_7_.1) | copy-start | bytes 393220
  67.6 4.3 %collective-permute-start.6 = (f32[5,8,2048]{2,1,0:T(8,128)S(1)}, f32[5,8,2048]{2,1,0:T(8,128)S(1)}, u32[]{:S(2)}, u32[]{:S(2)}) collective-permute-start(f32[5,8,2048]{2,1,0:T(8,128)S(1)} %get-tuple-element.17.refs_1_), channel_id=1, source_target_pairs={{0,1},{1,0},{2,3},{3,2},{4,5},{5,4},{6,7},{7,6},{8,9},{9,8},{10,11... | collective-permute-start | bytes 983048 | tf_op jit(solution)/shard_map/ppermute | solution.py:460
  68.4 3.5 %collective-permute-start.7 = (f32[5,8,2048]{2,1,0:T(8,128)S(1)}, f32[5,8,2048]{2,1,0:T(8,128)S(1)}, u32[]{:S(2)}, u32[]{:S(2)}) collective-permute-start(f32[5,8,2048]{2,1,0:T(8,128)S(1)} %get-tuple-element.17.refs_1_), channel_id=1, source_target_pairs={{1,2},{2,1},{3,4},{4,3},{5,6},{6,5},{7,8},{8,7},{9,10},{10,9},{11,... | collective-permute-start | bytes 983048 | tf_op jit(solution)/shard_map/ppermute | solution.py:460
  69.1 12.5 %collective-permute-start.10 = (f32[4,8,2048]{2,1,0:T(8,128)S(1)}, f32[4,8,2048]{2,1,0:T(8,128)S(1)}, u32[]{:S(2)}, u32[]{:S(2)}) collective-permute-start(f32[4,8,2048]{2,1,0:T(8,128)S(1)} %get-tuple-element.21), channel_id=1, source_target_pairs={{512,513},{513,514},{514,515},{515,516},{516,517},{517,518},{518,5... | collective-permute-start | bytes 786440 | tf_op jit(solution)/shard_map/ppermute | solution.py:517
  72.0 29.2 %collective-permute-start.9 = (f32[3,8,2048]{2,1,0:T(8,128)S(1)}, f32[3,8,2048]{2,1,0:T(8,128)S(1)}, u32[]{:S(2)}, u32[]{:S(2)}) collective-permute-start(f32[3,8,2048]{2,1,0:T(8,128)S(1)} %get-tuple-element.20.average), channel_id=1, source_target_pairs={{0,513},{1,514},{2,515},{3,516},{4,517},{5,518},{6,519},{7,520},{8... | collective-permute-start | bytes 589832 | tf_op jit(solution)/shard_map/ppermute | solution.py:520
  73.3 36.7 %collective-permute-start.8 = (f32[3,8,2048]{2,1,0:T(8,128)S(1)}, f32[3,8,2048]{2,1,0:T(8,128)S(1)}, u32[]{:S(2)}, u32[]{:S(2)}) collective-permute-start(f32[3,8,2048]{2,1,0:T(8,128)S(1)} %shard_map.82), channel_id=1, source_target_pairs={{0,512},{1,513},{2,514},{3,515},{4,516},{5,517},{6,518},{7,519},{8... | collective-permute-start | bytes 589832 | tf_op jit(solution)/shard_map/ppermute | solution.py:538

commit v3 on v2

--- a/solution.py
+++ b/solution.py
@@ -89,7 +89,7 @@
     def kernel(*refs):
         refs = list(refs)
         flag = refs.pop(0)
-        own, near, far = refs[:3]
+        own, far, near = refs[:3]
         refs = refs[3:]
         if first:
             targets, weights = refs[:2]
@@ -494,7 +494,7 @@
         kinds = (0, 1) if active else (0,)
         near = swapped(block, kinds, 0)
         far = swapped(block, kinds, 1)
-        operands = [flag, block, near, far]
+        operands = [flag, block, far, near]
         outs = [shape(5, rows, columns), shape(3, rows, columns)]
         operands += [targets, weights] if first else [stat, total]
         if last:

time: 111 us -> 103 us (0.928)
  starting transfers between devices: 40.3 us -> 35.8 us
  waiting for transfers between devices: 38.3 us -> 34.5 us
    ppermute x1, waiting for transfers between devices: 19.5 us -> 10.5 us  [body(): lax.ppermute(average, both, [(b, strips + (b + 1) % strips) for b in rang...]
    ppermute x8, starting transfers between devices: 35.8 us -> 31.3 us  [swapped(): return lax.ppermute(value, both, pairs)]
    ppermute x8, waiting for transfers between devices: 11.7 us -> 15 us  [swapped(): return lax.ppermute(value, both, pairs)]
    ppermute x1, waiting for transfers between devices: 7.08 us -> 9.06 us  [body(): lax.ppermute(links, both, [(strips + b, strips + (b + 1) % strips) for b...]
  transfers between devices with their start and end apart: 11 -> 11, of which waited for: 4 -> 5; matrix products, arithmetic and copies ran while one was open for 1% -> 1% of each run, Pallas kernels for 8% -> 9%
where the time goes in v3:
time: 103 us
  starting transfers between devices  35.8 us (35%)
  waiting for transfers between devices  34.5 us (33%)
  Pallas kernels  30.6 us (30%)
    ppermute x8, starting transfers between devices, swapped(): return lax.ppermute(value, both, pairs)  31.3 us
    ppermute x8, waiting for transfers between devices, swapped(): return lax.ppermute(value, both, pairs)  15 us
    pallas_call x1, Pallas kernels, body(): pl.pallas_call(partial(prep_kernel, strips), compiler_params=LIMITED, out...  13.2 us
    ppermute x1, waiting for transfers between devices, body(): lax.ppermute(average, both, [(b, strips + (b + 1) % strips) for b in rang...  10.5 us
    ppermute x1, waiting for transfers between devices, body(): lax.ppermute(links, both, [(strips + b, strips + (b + 1) % strips) for b...  9.06 us
    pallas_call x2, Pallas kernels, scattered(): pl.pallas_call(partial(kernel, strips), compiler_params=LIMITED, out_shap...  8.8 us
    pallas_call x4, Pallas kernels, body(): pl.pallas_call(make_round(strips, first, last, active, rows, tiles), comp...  7.69 us
  transfers between devices with their start and end apart: 11, of which 5 were waited for; matrix products, arithmetic and copies ran while one was open for 1% of the time, Pallas kernels for 9%

profile of v3, /device:TPU:65, one launch (start us, length us, event | category | flops | bytes accessed | tf_op | source)
XLA Modules:
  0.0 102.5 jit_solution(9130394126175590812)
XLA Ops:
  0.6 0.0 copy-start
  0.6 0.0 copy-start.1
  0.7 13.2 %shard_map.77.refs_1_ = f32[9,8,2048]{2,1,0:T(8,128)S(1)} custom-call(s32[1]{0:T(128)} %bitcast.flag.refs_0_, f32[1,5,8,2048]{3,2,1,0:T(8,128)} %refs_0_.1, f32[5,8,2048]{2,1,0:T(8,128)} %refs_1_.1, f32[2,8,2048]{2,1,0:T(8,128)} %refs_7_.1, s32[8,2048]{1,0:T(8,128)} %refs_8_.1), custom_call_target="tpu_custom_call" | custom-call | tf_op jit(solution)/shard_map/pallas_call | solution.py:468
  13.9 19.1 %collective-permute-start = (f32[9,8,2048]{2,1,0:T(8,128)S(1)}, f32[9,8,2048]{2,1,0:T(8,128)S(1)}, u32[]{:S(2)}, u32[]{:S(2)}) collective-permute-start(f32[9,8,2048]{2,1,0:T(8,128)S(1)} %shard_map.77.refs_1_), channel_id=1, source_target_pairs={{1,2},{2,1},{3,4},{4,3},{5,6},{6,5},{7,8},{8,7},{9,10},{10,9},{11,... | collective-permute-start | bytes 1769480 | tf_op jit(solution)/shard_map/ppermute | solution.py:460
  33.0 1.9 %collective-permute-start.1 = (f32[9,8,2048]{2,1,0:T(8,128)S(1)}, f32[9,8,2048]{2,1,0:T(8,128)S(1)}, u32[]{:S(2)}, u32[]{:S(2)}) collective-permute-start(f32[9,8,2048]{2,1,0:T(8,128)S(1)} %shard_map.77.refs_1_), channel_id=1, source_target_pairs={{0,1},{1,0},{2,3},{3,2},{4,5},{5,4},{6,7},{7,6},{8,9},{9,8},{10,11... | collective-permute-start | bytes 1769480 | tf_op jit(solution)/shard_map/ppermute | solution.py:460
  34.9 5.3 %collective-permute-done.refs_2_ = f32[9,8,2048]{2,1,0:T(8,128)S(1)} collective-permute-done((f32[9,8,2048]{2,1,0:T(8,128)S(1)}, f32[9,8,2048]{2,1,0:T(8,128)S(1)}, u32[]{:S(2)}, u32[]{:S(2)}) %collective-permute-start) | collective-permute-done | bytes 589856 | tf_op jit(solution)/shard_map/ppermute | solution.py:460
  40.3 3.4 %collective-permute-done.1.refs_3_ = f32[9,8,2048]{2,1,0:T(8,128)S(1)} collective-permute-done((f32[9,8,2048]{2,1,0:T(8,128)S(1)}, f32[9,8,2048]{2,1,0:T(8,128)S(1)}, u32[]{:S(2)}, u32[]{:S(2)}) %collective-permute-start.1) | collective-permute-done | bytes 589856 | tf_op jit(solution)/shard_map/ppermute | solution.py:460
  43.6 0.0 copy-done
  43.6 0.0 copy-done.1
  43.6 3.6 %shard_map.78 = (f32[5,8,2048]{2,1,0:T(8,128)S(1)}, f32[3,8,2048]{2,1,0:T(8,128)S(1)}, f32[4,16,24,128]{3,2,1,0:T(8,128)S(1)}, f32[4,8,2048]{2,1,0:T(8,128)S(1)}) custom-call(s32[1]{0:T(128)} %bitcast.flag.refs_0_, f32[9,8,2048]{2,1,0:T(8,128)S(1)} %shard_map.77.refs_1_, f32[9,8,2048]{2,1,0:T(8,128)S(1)} %collective-permute-done.refs_2_, ...), custom_call_target="tpu_custom_call" | custom-call | tf_op jit(solution)/shard_map/pallas_call | solution.py:504
  47.3 0.7 collective-permute-start.2
  48.0 0.7 collective-permute-start.3
  48.7 0.0 collective-permute-done.2.refs_2_
  48.7 0.0 collective-permute-done.3.refs_3_
  48.7 5.4 %collective-permute-start.4 = (f32[5,8,2048]{2,1,0:T(8,128)S(1)}, f32[5,8,2048]{2,1,0:T(8,128)S(1)}, u32[]{:S(2)}, u32[]{:S(2)}) collective-permute-start(f32[5,8,2048]{2,1,0:T(8,128)S(1)} %get-tuple-element.15.refs_1_), channel_id=1, source_target_pairs={{1,2},{2,1},{3,4},{4,3},{5,6},{6,5},{7,8},{8,7},{9,10},{10,9},{11,... | collective-permute-start | bytes 983048 | tf_op jit(solution)/shard_map/ppermute | solution.py:460
  54.2 1.9 %collective-permute-start.5 = (f32[5,8,2048]{2,1,0:T(8,128)S(1)}, f32[5,8,2048]{2,1,0:T(8,128)S(1)}, u32[]{:S(2)}, u32[]{:S(2)}) collective-permute-start(f32[5,8,2048]{2,1,0:T(8,128)S(1)} %get-tuple-element.15.refs_1_), channel_id=1, source_target_pairs={{0,1},{1,0},{2,3},{3,2},{4,5},{5,4},{6,7},{7,6},{8,9},{9,8},{10,11... | collective-permute-start | bytes 983048 | tf_op jit(solution)/shard_map/ppermute | solution.py:460
  56.1 6.3 %collective-permute-done.4.refs_2_ = f32[5,8,2048]{2,1,0:T(8,128)S(1)} collective-permute-done((f32[5,8,2048]{2,1,0:T(8,128)S(1)}, f32[5,8,2048]{2,1,0:T(8,128)S(1)}, u32[]{:S(2)}, u32[]{:S(2)}) %collective-permute-start.4) | collective-permute-done | bytes 327712 | tf_op jit(solution)/shard_map/ppermute | solution.py:460
  62.4 0.0 collective-permute-done.5.refs_3_
  62.4 0.0 copy-start.3
  62.4 4.0 %shard_map.80 = (f32[5,8,2048]{2,1,0:T(8,128)S(1)}, f32[3,8,2048]{2,1,0:T(8,128)S(1)}) custom-call(s32[1]{0:T(128)} %bitcast.flag.refs_0_, f32[5,8,2048]{2,1,0:T(8,128)S(1)} %get-tuple-element.15.refs_1_, f32[5,8,2048]{2,1,0:T(8,128)S(1)} %collective-permute-done.4.refs_2_, f32[5,8,2048]{2,1,0:T(8,128)S(1)} %collective-permute-done.5.refs_3_, ...), custom_call_target="tpu_custom_call" | custom-call | tf_op jit(solution)/shard_map/pallas_call | solution.py:504
  66.4 0.0 copy-start.2
  66.4 0.8 collective-permute-start.6
  67.2 0.7 collective-permute-start.7
  67.9 1.9 %collective-permute-start.10 = (f32[4,8,2048]{2,1,0:T(8,128)S(1)}, f32[4,8,2048]{2,1,0:T(8,128)S(1)}, u32[]{:S(2)}, u32[]{:S(2)}) collective-permute-start(f32[4,8,2048]{2,1,0:T(8,128)S(1)} %get-tuple-element.21), channel_id=1, source_target_pairs={{512,513},{513,514},{514,515},{515,516},{516,517},{517,518},{518,5... | collective-permute-start | bytes 786440 | tf_op jit(solution)/shard_map/ppermute | solution.py:517
  69.8 0.8 slice.3.refs_6_
  70.7 0.0 collective-permute-done.6.refs_2_
  70.7 0.0 collective-permute-done.7.refs_3_
  70.7 0.0 copy-done.3
  70.7 0.0 copy-done.2
  70.8 1.3 %collective-permute-start.9 = (f32[3,8,2048]{2,1,0:T(8,128)S(1)}, f32[3,8,2048]{2,1,0:T(8,128)S(1)}, u32[]{:S(2)}, u32[]{:S(2)}) collective-permute-start(f32[3,8,2048]{2,1,0:T(8,128)S(1)} %get-tuple-element.20.average), channel_id=1, source_target_pairs={{0,513},{1,514},{2,515},{3,516},{4,517},{5,518},{6,519},{7,520},{8... | collective-permute-start | bytes 589832 | tf_op jit(solution)/shard_map/ppermute | solution.py:520
  72.1 1.3 %collective-permute-start.8 = (f32[3,8,2048]{2,1,0:T(8,128)S(1)}, f32[3,8,2048]{2,1,0:T(8,128)S(1)}, u32[]{:S(2)}, u32[]{:S(2)}) collective-permute-start(f32[3,8,2048]{2,1,0:T(8,128)S(1)} %shard_map.82), channel_id=1, source_target_pairs={{0,512},{1,513},{2,514},{3,515},{4,516},{5,517},{6,518},{7,519},{8... | collective-permute-start | bytes 589832 | tf_op jit(solution)/shard_map/ppermute | solution.py:538
  73.4 9.1 %collective-permute-done.10.links = f32[4,8,2048]{2,1,0:T(8,128)S(1)} collective-permute-done((f32[4,8,2048]{2,1,0:T(8,128)S(1)}, f32[4,8,2048]{2,1,0:T(8,128)S(1)}, u32[]{:S(2)}, u32[]{:S(2)}) %collective-permute-start.10) | collective-permute-done | bytes 262176 | tf_op jit(solution)/shard_map/ppermute | solution.py:517
  82.4 10.5 %collective-permute-done.9.before = f32[3,8,2048]{2,1,0:T(8,128)S(1)} collective-permute-done((f32[3,8,2048]{2,1,0:T(8,128)S(1)}, f32[3,8,2048]{2,1,0:T(8,128)S(1)}, u32[]{:S(2)}, u32[]{:S(2)}) %collective-permute-start.9) | collective-permute-done | bytes 196640 | tf_op jit(solution)/shard_map/ppermute | solution.py:520
  92.9 8.8 %shard_map.83.upper = f32[3,8,2048]{2,1,0:T(8,128)S(1)} custom-call(s32[1]{0:T(128)} %bitcast.flag.refs_0_, f32[3,8,2048]{2,1,0:T(8,128)S(1)} %collective-permute-done.9.before, f32[4,8,2048]{2,1,0:T(8,128)S(1)} %collective-permute-done.10.links), custom_call_target="tpu_custom_call" | custom-call | tf_op jit(solution)/shard_map/pallas_call | solution.py:528
  101.7 0.0 collective-permute-done.8.lower
  101.7 0.8 shard_map.84
  (3 shorter events, 0.1 us)
Async XLA Ops:
  0.6 43.0 %copy-start = (s32[2,8,2048]{2,1,0:T(8,128)S(1)}, s32[2,8,2048]{2,1,0:T(8,128)}, u32[]{:S(2)}) copy-start(s32[2,8,2048]{2,1,0:T(8,128)} %targets.1) | copy-start | bytes 393220
  0.6 43.0 %copy-start.1 = (s32[2,8,2048]{2,1,0:T(8,128)S(1)}, s32[2,8,2048]{2,1,0:T(8,128)}, u32[]{:S(2)}) copy-start(s32[2,8,2048]{2,1,0:T(8,128)} %weights.1) | copy-start | bytes 393220
  13.9 26.4 %collective-permute-start = (f32[9,8,2048]{2,1,0:T(8,128)S(1)}, f32[9,8,2048]{2,1,0:T(8,128)S(1)}, u32[]{:S(2)}, u32[]{:S(2)}) collective-permute-start(f32[9,8,2048]{2,1,0:T(8,128)S(1)} %shard_map.77.refs_1_), channel_id=1, source_target_pairs={{1,2},{2,1},{3,4},{4,3},{5,6},{6,5},{7,8},{8,7},{9,10},{10,9},{11,... | collective-permute-start | bytes 1769480 | tf_op jit(solution)/shard_map/ppermute | solution.py:460
  33.0 10.6 %collective-permute-start.1 = (f32[9,8,2048]{2,1,0:T(8,128)S(1)}, f32[9,8,2048]{2,1,0:T(8,128)S(1)}, u32[]{:S(2)}, u32[]{:S(2)}) collective-permute-start(f32[9,8,2048]{2,1,0:T(8,128)S(1)} %shard_map.77.refs_1_), channel_id=1, source_target_pairs={{0,1},{1,0},{2,3},{3,2},{4,5},{5,4},{6,7},{7,6},{8,9},{9,8},{10,11... | collective-permute-start | bytes 1769480 | tf_op jit(solution)/shard_map/ppermute | solution.py:460
  47.3 1.4 %collective-permute-start.2 = (f32[5,8,2048]{2,1,0:T(8,128)S(1)}, f32[5,8,2048]{2,1,0:T(8,128)S(1)}, u32[]{:S(2)}, u32[]{:S(2)}) collective-permute-start(f32[5,8,2048]{2,1,0:T(8,128)S(1)} %get-tuple-element.12.refs_1_), channel_id=1, source_target_pairs={{1,2},{2,1},{3,4},{4,3},{5,6},{6,5},{7,8},{8,7},{9,10},{10,9},{11,... | collective-permute-start | bytes 983048 | tf_op jit(solution)/shard_map/ppermute | solution.py:460
  48.0 0.7 collective-permute-start.3
  48.7 13.7 %collective-permute-start.4 = (f32[5,8,2048]{2,1,0:T(8,128)S(1)}, f32[5,8,2048]{2,1,0:T(8,128)S(1)}, u32[]{:S(2)}, u32[]{:S(2)}) collective-permute-start(f32[5,8,2048]{2,1,0:T(8,128)S(1)} %get-tuple-element.15.refs_1_), channel_id=1, source_target_pairs={{1,2},{2,1},{3,4},{4,3},{5,6},{6,5},{7,8},{8,7},{9,10},{10,9},{11,... | collective-permute-start | bytes 983048 | tf_op jit(solution)/shard_map/ppermute | solution.py:460
  54.2 8.2 %collective-permute-start.5 = (f32[5,8,2048]{2,1,0:T(8,128)S(1)}, f32[5,8,2048]{2,1,0:T(8,128)S(1)}, u32[]{:S(2)}, u32[]{:S(2)}) collective-permute-start(f32[5,8,2048]{2,1,0:T(8,128)S(1)} %get-tuple-element.15.refs_1_), channel_id=1, source_target_pairs={{0,1},{1,0},{2,3},{3,2},{4,5},{5,4},{6,7},{7,6},{8,9},{9,8},{10,11... | collective-permute-start | bytes 983048 | tf_op jit(solution)/shard_map/ppermute | solution.py:460
  62.4 8.3 %copy-start.3 = (s32[8,2048]{1,0:T(8,128)S(1)}, s32[8,2048]{1,0:T(8,128)}, u32[]{:S(2)}) copy-start(s32[8,2048]{1,0:T(8,128)} %refs_8_.1) | copy-start | bytes 196612
  66.4 4.3 %copy-start.2 = (f32[2,8,2048]{2,1,0:T(8,128)S(1)}, f32[2,8,2048]{2,1,0:T(8,128)}, u32[]{:S(2)}) copy-start(f32[2,8,2048]{2,1,0:T(8,128)} %refs_7_.1) | copy-start | bytes 393220
  66.4 4.3 %collective-permute-start.6 = (f32[5,8,2048]{2,1,0:T(8,128)S(1)}, f32[5,8,2048]{2,1,0:T(8,128)S(1)}, u32[]{:S(2)}, u32[]{:S(2)}) collective-permute-start(f32[5,8,2048]{2,1,0:T(8,128)S(1)} %get-tuple-element.17.refs_1_), channel_id=1, source_target_pairs={{1,2},{2,1},{3,4},{4,3},{5,6},{6,5},{7,8},{8,7},{9,10},{10,9},{11,... | collective-permute-start | bytes 983048 | tf_op jit(solution)/shard_map/ppermute | solution.py:460
  67.2 3.5 %collective-permute-start.7 = (f32[5,8,2048]{2,1,0:T(8,128)S(1)}, f32[5,8,2048]{2,1,0:T(8,128)S(1)}, u32[]{:S(2)}, u32[]{:S(2)}) collective-permute-start(f32[5,8,2048]{2,1,0:T(8,128)S(1)} %get-tuple-element.17.refs_1_), channel_id=1, source_target_pairs={{0,1},{1,0},{2,3},{3,2},{4,5},{5,4},{6,7},{7,6},{8,9},{9,8},{10,11... | collective-permute-start | bytes 983048 | tf_op jit(solution)/shard_map/ppermute | solution.py:460
  67.9 14.5 %collective-permute-start.10 = (f32[4,8,2048]{2,1,0:T(8,128)S(1)}, f32[4,8,2048]{2,1,0:T(8,128)S(1)}, u32[]{:S(2)}, u32[]{:S(2)}) collective-permute-start(f32[4,8,2048]{2,1,0:T(8,128)S(1)} %get-tuple-element.21), channel_id=1, source_target_pairs={{512,513},{513,514},{514,515},{515,516},{516,517},{517,518},{518,5... | collective-permute-start | bytes 786440 | tf_op jit(solution)/shard_map/ppermute | solution.py:517
  70.8 22.1 %collective-permute-start.9 = (f32[3,8,2048]{2,1,0:T(8,128)S(1)}, f32[3,8,2048]{2,1,0:T(8,128)S(1)}, u32[]{:S(2)}, u32[]{:S(2)}) collective-permute-start(f32[3,8,2048]{2,1,0:T(8,128)S(1)} %get-tuple-element.20.average), channel_id=1, source_target_pairs={{0,513},{1,514},{2,515},{3,516},{4,517},{5,518},{6,519},{7,520},{8... | collective-permute-start | bytes 589832 | tf_op jit(solution)/shard_map/ppermute | solution.py:520
  72.1 29.6 %collective-permute-start.8 = (f32[3,8,2048]{2,1,0:T(8,128)S(1)}, f32[3,8,2048]{2,1,0:T(8,128)S(1)}, u32[]{:S(2)}, u32[]{:S(2)}) collective-permute-start(f32[3,8,2048]{2,1,0:T(8,128)S(1)} %shard_map.82), channel_id=1, source_target_pairs={{0,512},{1,513},{2,514},{3,515},{4,516},{5,517},{6,518},{7,519},{8... | collective-permute-start | bytes 589832 | tf_op jit(solution)/shard_map/ppermute | solution.py:538

commit v4 on v3

--- a/solution.py
+++ b/solution.py
@@ -31,10 +31,11 @@
 
 
 def prep_kernel(strips, flag, *refs):
-    sources, out, (initial, forcing, current, cover), arrived = refs[:4], refs[4], refs[5:9], refs[9]
+    sources, (out, extra), landed, arrived = refs[:6], refs[6:8], refs[8:14], refs[14]
+    initial, forcing, current, cover, targets, weights = landed
     copies = [
         pltpu.make_async_copy(source, target, arrived.at[i])
-        for i, (source, target) in enumerate(zip(sources, (initial, forcing, current, cover)))
+        for i, (source, target) in enumerate(zip(sources, landed))
     ]
     for copy in copies:
         copy.start()
@@ -54,6 +55,9 @@
         out[6] = g
         out[7] = g * (forcing[2] + drag_coef * current[0])
         out[8] = g * (forcing[3] + drag_coef * current[1])
+        extra[0] = covered * current[0]
+        extra[1] = covered * current[1]
+        extra[2] = covered * forcing[4]
 
     @pl.when(flag[0] >= strips)
     def _():
@@ -64,6 +68,9 @@
         out[6] = current[1]
         out[7] = jnp.zeros_like(current[0])
         out[8] = jnp.zeros_like(current[0])
+        for entry in range(2):
+            extra[entry] = targets[entry].astype(jnp.float32)
+            extra[2 + entry] = weights[entry].astype(jnp.float32)
 
 
 def load_strip(dst, dst_plane, src, src_plane, part, tiles, base):
@@ -91,17 +98,14 @@
         flag = refs.pop(0)
         own, far, near = refs[:3]
         refs = refs[3:]
+        if not first:
+            stat, total_in = refs[:2]
+            refs = refs[2:]
+        if last:
+            extra = refs.pop(0)
         if first:
-            targets, weights = refs[:2]
-        else:
-            stat, total_in = refs[:2]
-        refs = refs[2:]
-        if last:
-            melt, current, cover = refs[:3]
+            out, total, stat = refs[:3]
             refs = refs[3:]
-        if first:
-            out, total, stat, links = refs[:4]
-            refs = refs[4:]
         else:
             out, total = refs[:2]
             refs = refs[2:]
@@ -264,15 +268,12 @@
                         0.5 * (mine[2] - mine[3]),
                         0.5 * mine[4],
                     ]
-                    covered = cover[:, lanes].astype(jnp.float32)
-                    total[0, :, lanes] = (
-                        total[0, :, lanes] * (1.0 / SUBCYCLES) - covered * current[0, :, lanes]
-                    )
-                    total[1, :, lanes] = (
-                        total[1, :, lanes] * (1.0 / SUBCYCLES) - covered * current[1, :, lanes]
-                    )
+                    for part in range(2):
+                        total[part, :, lanes] = (
+                            total[part, :, lanes] * (1.0 / SUBCYCLES) - extra[part, :, lanes]
+                        )
                     total[2, :, lanes] = (
-                        total[2, :, lanes] * (melt[0, :, lanes] * covered) * (1.0 / SUBCYCLES)
+                        total[2, :, lanes] * extra[2, :, lanes] * (1.0 / SUBCYCLES)
                     )
                 for p in range(5):
                     out[p, :, lanes] = mine[p]
@@ -280,9 +281,6 @@
         def ocean():
             if first:
                 load_windows(stat, [(plane, 5 + plane) for plane in range(2)], (0, 0))
-                for entry in range(2):
-                    links[entry] = targets[entry].astype(jnp.float32)
-                    links[2 + entry] = weights[entry].astype(jnp.float32)
             if not ocean_active:
                 out[...] = own[:5]
                 return
@@ -349,7 +347,7 @@
 WIDE = 256
 
 
-def scatter_half(half, values, spots_of, weights_of, sums, blocks):
+def scatter_half(half, values, spots_of, weights_of, sums, blocks, rights=None):
     rows = values.shape[1]
     columns = values.shape[2]
     groups = columns // WIDE
@@ -361,7 +359,7 @@
     zero = jnp.zeros((), jnp.bfloat16)
     one = jnp.ones((), jnp.bfloat16)
 
-    def build(turn, left, right):
+    def build(turn, left, right=None):
         entry = turn // rows
         row = turn % rows
         spot = spots_of[entry, pl.ds(row, 1), :].astype(jnp.int32)
@@ -371,9 +369,10 @@
         inside = jnp.logical_and(high >= 0, high < spots)
         place = jnp.bitwise_and(high, groups - 1) * rows + high // groups
         place = jnp.where(inside, place, -1)
-        low = low.astype(jnp.float32).astype(jnp.bfloat16)
         place = place.astype(jnp.float32).astype(jnp.bfloat16)
-        right[...] = jnp.where(low_at == low, one, zero)
+        if right is not None:
+            low = low.astype(jnp.float32).astype(jnp.bfloat16)
+            right[...] = jnp.where(low_at == low, one, zero)
         hit = high_at == place
         for channel in range(3):
             value = values[channel, pl.ds(row, 1), :] * scale
@@ -391,14 +390,22 @@
             preferred_element_type=jnp.float32,
         )
 
-    left_a, right_a, left_b, right_b = blocks
+    if rights is None:
+        left_a, right_a, left_b, right_b = blocks
+    else:
+        left_a, left_b = blocks
+        right_a = right_b = None
+
+    def at(turn, right):
+        return right if rights is None else rights.at[turn]
+
     build(0, left_a, right_a)
 
     def step(pair, carry):
         build(2 * pair + 1, left_b, right_b)
-        multiply(left_a, right_a)
+        multiply(left_a, at(2 * pair, right_a))
         build(jnp.minimum(2 * pair + 2, turns - 1), left_a, right_a)
-        multiply(left_b, right_b)
+        multiply(left_b, at(2 * pair + 1, right_b))
         return carry
 
     lax.fori_loop(0, turns // 2, step, 0)
@@ -410,8 +417,8 @@
     return tile, groups
 
 
-def write_half(half, values, spots_of, weights_of, out, sums, blocks):
-    tile, groups = scatter_half(half, values, spots_of, weights_of, sums, blocks)
+def write_half(half, values, spots_of, weights_of, out, sums, blocks, rights=None):
+    tile, groups = scatter_half(half, values, spots_of, weights_of, sums, blocks, rights)
     for channel in range(3):
         for g in range(groups):
             out[channel, :, g * WIDE : (g + 1) * WIDE] = tile(channel, g)
@@ -423,10 +430,28 @@
         write_half(0, average, targets, weights, out, sums, blocks)
 
 
-def upper_kernel(strips, flag, before, links, out, sums, *blocks):
+def rights_kernel(strips, flag, links, out):
     @pl.when(flag[0] >= strips)
     def _():
-        write_half(1, before, links.at[:2], links.at[2:], out, sums, blocks)
+        turns, _, columns = out.shape
+        rows = turns // 2
+        low_at = lax.broadcasted_iota(jnp.int32, (WIDE, columns), 0).astype(jnp.bfloat16)
+
+        def step(turn, carry):
+            spot = links[turn // rows, pl.ds(turn % rows, 1), :].astype(jnp.int32)
+            low = jnp.bitwise_and(spot, WIDE - 1).astype(jnp.float32).astype(jnp.bfloat16)
+            out[turn] = jnp.where(
+                low_at == low, jnp.ones((), jnp.bfloat16), jnp.zeros((), jnp.bfloat16)
+            )
+            return carry
+
+        lax.fori_loop(0, turns, step, 0)
+
+
+def upper_kernel(strips, flag, before, links, rights, out, sums, *blocks):
+    @pl.when(flag[0] >= strips)
+    def _():
+        write_half(1, before, links.at[:2], links.at[2:], out, sums, blocks, rights)
 
 
 def final_kernel(strips, flag, fields, average, lower, upper, state, coupled):
@@ -465,24 +490,16 @@
     def held(*values):
         return [pltpu.with_memory_space_constraint(value, pltpu.VMEM) for value in values]
 
-    block = pl.pallas_call(
+    inputs = (initial, ice_forcing, ocean_current, ice_cover, targets, weights)
+    block, extra = pl.pallas_call(
         partial(prep_kernel, strips),
         compiler_params=LIMITED,
-        out_shape=shape(9, rows, columns),
-        in_specs=[SMEM] + [pl.BlockSpec(memory_space=pltpu.HBM)] * 4,
-        out_specs=VMEM,
-        scratch_shapes=[
-            pltpu.VMEM(value.shape, value.dtype)
-            for value in (initial, ice_forcing, ocean_current, ice_cover)
-        ]
-        + [pltpu.SemaphoreType.DMA((4,))],
-    )(
-        flag,
-        *(
-            pltpu.with_memory_space_constraint(value, pltpu.HBM)
-            for value in (initial, ice_forcing, ocean_current, ice_cover)
-        ),
-    )
+        out_shape=[shape(9, rows, columns), shape(4, rows, columns)],
+        in_specs=[SMEM] + [pl.BlockSpec(memory_space=pltpu.HBM)] * 6,
+        out_specs=[VMEM] * 2,
+        scratch_shapes=[pltpu.VMEM(value.shape, value.dtype) for value in inputs]
+        + [pltpu.SemaphoreType.DMA((6,))],
+    )(flag, *(pltpu.with_memory_space_constraint(value, pltpu.HBM) for value in inputs))
 
     rounds = SUBCYCLES // ICE_DEPTH
     each = OCEAN_DEPTH // ICE_DEPTH
@@ -496,11 +513,12 @@
         far = swapped(block, kinds, 1)
         operands = [flag, block, far, near]
         outs = [shape(5, rows, columns), shape(3, rows, columns)]
-        operands += [targets, weights] if first else [stat, total]
+        if not first:
+            operands += [stat, total]
         if last:
-            operands += [ice_forcing[4:], ocean_current, ice_cover]
+            operands.append(extra)
         if first:
-            outs += [shape(4, tiles, window, LANES), shape(4, rows, columns)]
+            outs.append(shape(4, tiles, window, LANES))
         done = pl.pallas_call(
             make_round(strips, first, last, active, rows, tiles),
             compiler_params=LIMITED,
@@ -511,20 +529,19 @@
         )(flag, *held(*operands[1:]))
         block, total = done[:2]
         if first:
-            stat, links = done[2:]
+            stat = done[2]
 
     average = total
     links_before = lax.ppermute(
-        links, both, [(strips + b, strips + (b + 1) % strips) for b in range(strips)]
+        extra, both, [(strips + b, strips + (b + 1) % strips) for b in range(strips)]
     )
     before = lax.ppermute(average, both, [(b, strips + (b + 1) % strips) for b in range(strips)])
     spots = rows * columns // WIDE
-    scratch = [pltpu.VMEM((6 * spots, WIDE), jnp.float32)] + [
-        pltpu.VMEM((6 * spots, columns), jnp.bfloat16),
-        pltpu.VMEM((WIDE, columns), jnp.bfloat16),
-    ] * 2
-
-    def scattered(kernel, *operands):
+    sums = pltpu.VMEM((6 * spots, WIDE), jnp.float32)
+    left = pltpu.VMEM((6 * spots, columns), jnp.bfloat16)
+    right = pltpu.VMEM((WIDE, columns), jnp.bfloat16)
+
+    def scattered(kernel, scratch, *operands):
         return pl.pallas_call(
             partial(kernel, strips),
             compiler_params=LIMITED,
@@ -534,9 +551,16 @@
             scratch_shapes=scratch,
         )(flag, *held(*operands))
 
-    lower = scattered(lower_kernel, average, targets, weights)
+    lower = scattered(lower_kernel, [sums, left, right, left, right], average, targets, weights)
     received = lax.ppermute(lower, both, [(b, strips + b) for b in range(strips)])
-    upper = scattered(upper_kernel, before, links_before)
+    rights = pl.pallas_call(
+        partial(rights_kernel, strips),
+        compiler_params=LIMITED,
+        out_shape=pltpu.VMEM((2 * rows, WIDE, columns), jnp.bfloat16),
+        in_specs=[SMEM, VMEM],
+        out_specs=VMEM,
+    )(flag, *held(links_before))
+    upper = scattered(upper_kernel, [sums, left, left], before, links_before, rights)
     return tuple(
         pl.pallas_call(
             partial(final_kernel, strips),

time: 103 us -> 103 us (level)
  waiting for transfers between devices: 34.5 us -> 31.5 us
  Pallas kernels: 30.6 us -> 32.5 us
    pallas_call x0 -> x1, Pallas kernels: none -> 2.05 us  [body(): pl.pallas_call(partial(rights_kernel, strips), compiler_params=LIMITED, o...]
    ppermute x1, waiting for transfers between devices: 10.5 us -> 8.42 us  [body(): lax.ppermute(average, both, [(b, strips + (b + 1) % strips) for b in rang...]
    unnamed x8 -> x4, local copies, waits for them, and re-layouts: 0.02 us -> 1.8 us
  transfers between devices with their start and end apart: 11 -> 11, of which waited for: 5 -> 5; matrix products, arithmetic and copies ran while one was open for 1% -> 0% of each run, Pallas kernels for 9% -> 10%
where the time goes in v4:
time: 103 us; the launch traced here: 102 us
  starting transfers between devices  35.6 us (35%)
  Pallas kernels  32.5 us (32%)
  waiting for transfers between devices  31.5 us (31%)
  local copies, waits for them, and re-layouts  1.8 us (2%)
    ppermute x8, starting transfers between devices, swapped(): return lax.ppermute(value, both, pairs)  31.1 us
    ppermute x8, waiting for transfers between devices, swapped(): return lax.ppermute(value, both, pairs)  15 us
    pallas_call x1, Pallas kernels, body(): pl.pallas_call(partial(prep_kernel, strips), compiler_params=LIMITED, out...  13.3 us
    pallas_call x2, Pallas kernels, scattered(): pl.pallas_call(partial(kernel, strips), compiler_params=LIMITED, out_shap...  8.6 us
    ppermute x1, waiting for transfers between devices, body(): lax.ppermute(average, both, [(b, strips + (b + 1) % strips) for b in rang...  8.42 us
    ppermute x1, waiting for transfers between devices, body(): lax.ppermute(extra, both, [(strips + b, strips + (b + 1) % strips) for b...  8.11 us
    pallas_call x4, Pallas kernels, body(): pl.pallas_call(make_round(strips, first, last, active, rows, tiles), comp...  7.67 us
  transfers between devices with their start and end apart: 11, of which 5 were waited for; matrix products, arithmetic and copies ran while one was open for 0% of the time, Pallas kernels for 10%

profile of v4, /device:TPU:65, one launch (start us, length us, event | category | flops | bytes accessed | tf_op | source)
XLA Modules:
  0.0 102.2 jit_solution(14074399999628633358)
XLA Ops:
  0.6 13.3 %shard_map.77 = (f32[9,8,2048]{2,1,0:T(8,128)S(1)}, f32[4,8,2048]{2,1,0:T(8,128)S(1)}) custom-call(s32[1]{0:T(128)} %bitcast.flag.refs_0_, f32[1,5,8,2048]{3,2,1,0:T(8,128)} %refs_0_.1, f32[5,8,2048]{2,1,0:T(8,128)} %refs_1_.1, f32[2,8,2048]{2,1,0:T(8,128)} %refs_2_.1, s32[8,2048]{1,0:T(8,128)} %refs_3_.1, s32[2,8,2048]{2,1,0:T(8,128)} %targets.1, ...), custom_call_target="tpu_custom_call" | custom-call | tf_op jit(solution)/shard_map/pallas_call | solution.py:494
  14.0 19.1 %collective-permute-start = (f32[9,8,2048]{2,1,0:T(8,128)S(1)}, f32[9,8,2048]{2,1,0:T(8,128)S(1)}, u32[]{:S(2)}, u32[]{:S(2)}) collective-permute-start(f32[9,8,2048]{2,1,0:T(8,128)S(1)} %get-tuple-element.13.refs_1_), channel_id=1, source_target_pairs={{1,2},{2,1},{3,4},{4,3},{5,6},{6,5},{7,8},{8,7},{9,10},{10,9},{11,... | collective-permute-start | bytes 1769480 | tf_op jit(solution)/shard_map/ppermute | solution.py:485
  33.1 1.9 %collective-permute-start.1 = (f32[9,8,2048]{2,1,0:T(8,128)S(1)}, f32[9,8,2048]{2,1,0:T(8,128)S(1)}, u32[]{:S(2)}, u32[]{:S(2)}) collective-permute-start(f32[9,8,2048]{2,1,0:T(8,128)S(1)} %get-tuple-element.13.refs_1_), channel_id=1, source_target_pairs={{0,1},{1,0},{2,3},{3,2},{4,5},{5,4},{6,7},{7,6},{8,9},{9,8},{10,11... | collective-permute-start | bytes 1769480 | tf_op jit(solution)/shard_map/ppermute | solution.py:485
  35.0 5.3 %collective-permute-done.refs_2_ = f32[9,8,2048]{2,1,0:T(8,128)S(1)} collective-permute-done((f32[9,8,2048]{2,1,0:T(8,128)S(1)}, f32[9,8,2048]{2,1,0:T(8,128)S(1)}, u32[]{:S(2)}, u32[]{:S(2)}) %collective-permute-start) | collective-permute-done | bytes 589856 | tf_op jit(solution)/shard_map/ppermute | solution.py:485
  40.3 3.4 %collective-permute-done.1.refs_3_ = f32[9,8,2048]{2,1,0:T(8,128)S(1)} collective-permute-done((f32[9,8,2048]{2,1,0:T(8,128)S(1)}, f32[9,8,2048]{2,1,0:T(8,128)S(1)}, u32[]{:S(2)}, u32[]{:S(2)}) %collective-permute-start.1) | collective-permute-done | bytes 589856 | tf_op jit(solution)/shard_map/ppermute | solution.py:485
  43.7 3.6 %shard_map.78 = (f32[5,8,2048]{2,1,0:T(8,128)S(1)}, f32[3,8,2048]{2,1,0:T(8,128)S(1)}, f32[4,16,24,128]{3,2,1,0:T(8,128)S(1)}) custom-call(s32[1]{0:T(128)} %bitcast.flag.refs_0_, f32[9,8,2048]{2,1,0:T(8,128)S(1)} %get-tuple-element.13.refs_1_, f32[9,8,2048]{2,1,0:T(8,128)S(1)} %collective-permute-done.refs_2_, f32[9,8,2048]{2,1,0:T(8,128)S(1)} %collective-permute-done.1.refs_3_), custom_call_target="tpu_custom_call" | custom-call | tf_op jit(solution)/shard_map/pallas_call | solution.py:522
  47.3 0.7 collective-permute-start.2
  48.0 0.7 collective-permute-start.3
  48.7 0.0 collective-permute-done.2.refs_2_
  48.7 0.0 collective-permute-done.3.refs_3_
  48.8 5.4 %collective-permute-start.4 = (f32[5,8,2048]{2,1,0:T(8,128)S(1)}, f32[5,8,2048]{2,1,0:T(8,128)S(1)}, u32[]{:S(2)}, u32[]{:S(2)}) collective-permute-start(f32[5,8,2048]{2,1,0:T(8,128)S(1)} %get-tuple-element.17.refs_1_), channel_id=1, source_target_pairs={{1,2},{2,1},{3,4},{4,3},{5,6},{6,5},{7,8},{8,7},{9,10},{10,9},{11,... | collective-permute-start | bytes 983048 | tf_op jit(solution)/shard_map/ppermute | solution.py:485
  54.2 1.9 %collective-permute-start.5 = (f32[5,8,2048]{2,1,0:T(8,128)S(1)}, f32[5,8,2048]{2,1,0:T(8,128)S(1)}, u32[]{:S(2)}, u32[]{:S(2)}) collective-permute-start(f32[5,8,2048]{2,1,0:T(8,128)S(1)} %get-tuple-element.17.refs_1_), channel_id=1, source_target_pairs={{0,1},{1,0},{2,3},{3,2},{4,5},{5,4},{6,7},{7,6},{8,9},{9,8},{10,11... | collective-permute-start | bytes 983048 | tf_op jit(solution)/shard_map/ppermute | solution.py:485
  56.1 6.3 %collective-permute-done.4.refs_2_ = f32[5,8,2048]{2,1,0:T(8,128)S(1)} collective-permute-done((f32[5,8,2048]{2,1,0:T(8,128)S(1)}, f32[5,8,2048]{2,1,0:T(8,128)S(1)}, u32[]{:S(2)}, u32[]{:S(2)}) %collective-permute-start.4) | collective-permute-done | bytes 327712 | tf_op jit(solution)/shard_map/ppermute | solution.py:485
  62.4 0.0 collective-permute-done.5.refs_3_
  62.4 4.0 %shard_map.80 = (f32[5,8,2048]{2,1,0:T(8,128)S(1)}, f32[3,8,2048]{2,1,0:T(8,128)S(1)}) custom-call(s32[1]{0:T(128)} %bitcast.flag.refs_0_, f32[5,8,2048]{2,1,0:T(8,128)S(1)} %get-tuple-element.17.refs_1_, f32[5,8,2048]{2,1,0:T(8,128)S(1)} %collective-permute-done.4.refs_2_, f32[5,8,2048]{2,1,0:T(8,128)S(1)} %collective-permute-done.5.refs_3_, ...), custom_call_target="tpu_custom_call" | custom-call | tf_op jit(solution)/shard_map/pallas_call | solution.py:522
  66.4 0.7 collective-permute-start.6
  67.1 0.7 collective-permute-start.7
  67.8 1.9 %collective-permute-start.10 = (f32[4,8,2048]{2,1,0:T(8,128)S(1)}, f32[4,8,2048]{2,1,0:T(8,128)S(1)}, u32[]{:S(2)}, u32[]{:S(2)}) collective-permute-start(f32[4,8,2048]{2,1,0:T(8,128)S(1)} %get-tuple-element.21.refs_6_), channel_id=1, source_target_pairs={{512,513},{513,514},{514,515},{515,516},{516,517},{517,518},{518,5... | collective-permute-start | bytes 786440 | tf_op jit(solution)/shard_map/ppermute | solution.py:535
  69.7 0.0 collective-permute-done.6.refs_2_
  69.7 0.0 collective-permute-done.7.refs_3_
  69.8 1.3 %collective-permute-start.9 = (f32[3,8,2048]{2,1,0:T(8,128)S(1)}, f32[3,8,2048]{2,1,0:T(8,128)S(1)}, u32[]{:S(2)}, u32[]{:S(2)}) collective-permute-start(f32[3,8,2048]{2,1,0:T(8,128)S(1)} %get-tuple-element.23.average), channel_id=1, source_target_pairs={{0,513},{1,514},{2,515},{3,516},{4,517},{5,518},{6,519},{7,520},{8... | collective-permute-start | bytes 589832 | tf_op jit(solution)/shard_map/ppermute | solution.py:538
  71.1 0.0 copy-start
  71.1 0.9 copy-done
  72.0 0.0 copy-start.1
  72.0 0.9 copy-done.1
  72.9 1.3 %collective-permute-start.8 = (f32[3,8,2048]{2,1,0:T(8,128)S(1)}, f32[3,8,2048]{2,1,0:T(8,128)S(1)}, u32[]{:S(2)}, u32[]{:S(2)}) collective-permute-start(f32[3,8,2048]{2,1,0:T(8,128)S(1)} %shard_map.82), channel_id=1, source_target_pairs={{0,512},{1,513},{2,514},{3,515},{4,516},{5,517},{6,518},{7,519},{8... | collective-permute-start | bytes 589832 | tf_op jit(solution)/shard_map/ppermute | solution.py:555
  74.2 8.1 %collective-permute-done.10.links = f32[4,8,2048]{2,1,0:T(8,128)S(1)} collective-permute-done((f32[4,8,2048]{2,1,0:T(8,128)S(1)}, f32[4,8,2048]{2,1,0:T(8,128)S(1)}, u32[]{:S(2)}, u32[]{:S(2)}) %collective-permute-start.10) | collective-permute-done | bytes 262176 | tf_op jit(solution)/shard_map/ppermute | solution.py:535
  82.3 2.0 %shard_map.83.rights = bf16[16,256,2048]{2,1,0:T(8,128)(2,1)S(1)} custom-call(s32[1]{0:T(128)} %bitcast.flag.refs_0_, f32[4,8,2048]{2,1,0:T(8,128)S(1)} %collective-permute-done.10.links), custom_call_target="tpu_custom_call" | custom-call | tf_op jit(solution)/shard_map/pallas_call | solution.py:556
  84.4 8.4 %collective-permute-done.9.before = f32[3,8,2048]{2,1,0:T(8,128)S(1)} collective-permute-done((f32[3,8,2048]{2,1,0:T(8,128)S(1)}, f32[3,8,2048]{2,1,0:T(8,128)S(1)}, u32[]{:S(2)}, u32[]{:S(2)}) %collective-permute-start.9) | collective-permute-done | bytes 196640 | tf_op jit(solution)/shard_map/ppermute | solution.py:538
  92.8 8.6 %shard_map.84.upper = f32[3,8,2048]{2,1,0:T(8,128)S(1)} custom-call(s32[1]{0:T(128)} %bitcast.flag.refs_0_, f32[3,8,2048]{2,1,0:T(8,128)S(1)} %collective-permute-done.9.before, f32[4,8,2048]{2,1,0:T(8,128)S(1)} %collective-permute-done.10.links, bf16[16,256,2048]{2,1,0:T(8,128)(2,1)S(1)} %shard_map.83.rights), custom_call_target="tpu_custom_call" | custom-call | tf_op jit(solution)/shard_map/pallas_call | solution.py:545
  101.4 0.0 collective-permute-done.8.lower
  101.4 0.8 shard_map.85
  (3 shorter events, 0.1 us)
Async XLA Ops:
  14.0 26.4 %collective-permute-start = (f32[9,8,2048]{2,1,0:T(8,128)S(1)}, f32[9,8,2048]{2,1,0:T(8,128)S(1)}, u32[]{:S(2)}, u32[]{:S(2)}) collective-permute-start(f32[9,8,2048]{2,1,0:T(8,128)S(1)} %get-tuple-element.13.refs_1_), channel_id=1, source_target_pairs={{1,2},{2,1},{3,4},{4,3},{5,6},{6,5},{7,8},{8,7},{9,10},{10,9},{11,... | collective-permute-start | bytes 1769480 | tf_op jit(solution)/shard_map/ppermute | solution.py:485
  33.1 10.6 %collective-permute-start.1 = (f32[9,8,2048]{2,1,0:T(8,128)S(1)}, f32[9,8,2048]{2,1,0:T(8,128)S(1)}, u32[]{:S(2)}, u32[]{:S(2)}) collective-permute-start(f32[9,8,2048]{2,1,0:T(8,128)S(1)} %get-tuple-element.13.refs_1_), channel_id=1, source_target_pairs={{0,1},{1,0},{2,3},{3,2},{4,5},{5,4},{6,7},{7,6},{8,9},{9,8},{10,11... | collective-permute-start | bytes 1769480 | tf_op jit(solution)/shard_map/ppermute | solution.py:485
  47.3 1.4 %collective-permute-start.2 = (f32[5,8,2048]{2,1,0:T(8,128)S(1)}, f32[5,8,2048]{2,1,0:T(8,128)S(1)}, u32[]{:S(2)}, u32[]{:S(2)}) collective-permute-start(f32[5,8,2048]{2,1,0:T(8,128)S(1)} %get-tuple-element.14.refs_1_), channel_id=1, source_target_pairs={{1,2},{2,1},{3,4},{4,3},{5,6},{6,5},{7,8},{8,7},{9,10},{10,9},{11,... | collective-permute-start | bytes 983048 | tf_op jit(solution)/shard_map/ppermute | solution.py:485
  48.0 0.7 collective-permute-start.3
  48.8 13.7 %collective-permute-start.4 = (f32[5,8,2048]{2,1,0:T(8,128)S(1)}, f32[5,8,2048]{2,1,0:T(8,128)S(1)}, u32[]{:S(2)}, u32[]{:S(2)}) collective-permute-start(f32[5,8,2048]{2,1,0:T(8,128)S(1)} %get-tuple-element.17.refs_1_), channel_id=1, source_target_pairs={{1,2},{2,1},{3,4},{4,3},{5,6},{6,5},{7,8},{8,7},{9,10},{10,9},{11,... | collective-permute-start | bytes 983048 | tf_op jit(solution)/shard_map/ppermute | solution.py:485
  54.2 8.2 %collective-permute-start.5 = (f32[5,8,2048]{2,1,0:T(8,128)S(1)}, f32[5,8,2048]{2,1,0:T(8,128)S(1)}, u32[]{:S(2)}, u32[]{:S(2)}) collective-permute-start(f32[5,8,2048]{2,1,0:T(8,128)S(1)} %get-tuple-element.17.refs_1_), channel_id=1, source_target_pairs={{0,1},{1,0},{2,3},{3,2},{4,5},{5,4},{6,7},{7,6},{8,9},{9,8},{10,11... | collective-permute-start | bytes 983048 | tf_op jit(solution)/shard_map/ppermute | solution.py:485
  66.4 3.3 %collective-permute-start.6 = (f32[5,8,2048]{2,1,0:T(8,128)S(1)}, f32[5,8,2048]{2,1,0:T(8,128)S(1)}, u32[]{:S(2)}, u32[]{:S(2)}) collective-permute-start(f32[5,8,2048]{2,1,0:T(8,128)S(1)} %get-tuple-element.19.refs_1_), channel_id=1, source_target_pairs={{1,2},{2,1},{3,4},{4,3},{5,6},{6,5},{7,8},{8,7},{9,10},{10,9},{11,... | collective-permute-start | bytes 983048 | tf_op jit(solution)/shard_map/ppermute | solution.py:485
  67.1 2.6 %collective-permute-start.7 = (f32[5,8,2048]{2,1,0:T(8,128)S(1)}, f32[5,8,2048]{2,1,0:T(8,128)S(1)}, u32[]{:S(2)}, u32[]{:S(2)}) collective-permute-start(f32[5,8,2048]{2,1,0:T(8,128)S(1)} %get-tuple-element.19.refs_1_), channel_id=1, source_target_pairs={{0,1},{1,0},{2,3},{3,2},{4,5},{5,4},{6,7},{7,6},{8,9},{9,8},{10,11... | collective-permute-start | bytes 983048 | tf_op jit(solution)/shard_map/ppermute | solution.py:485
  67.8 14.5 %collective-permute-start.10 = (f32[4,8,2048]{2,1,0:T(8,128)S(1)}, f32[4,8,2048]{2,1,0:T(8,128)S(1)}, u32[]{:S(2)}, u32[]{:S(2)}) collective-permute-start(f32[4,8,2048]{2,1,0:T(8,128)S(1)} %get-tuple-element.21.refs_6_), channel_id=1, source_target_pairs={{512,513},{513,514},{514,515},{515,516},{516,517},{517,518},{518,5... | collective-permute-start | bytes 786440 | tf_op jit(solution)/shard_map/ppermute | solution.py:535
  69.8 23.0 %collective-permute-start.9 = (f32[3,8,2048]{2,1,0:T(8,128)S(1)}, f32[3,8,2048]{2,1,0:T(8,128)S(1)}, u32[]{:S(2)}, u32[]{:S(2)}) collective-permute-start(f32[3,8,2048]{2,1,0:T(8,128)S(1)} %get-tuple-element.23.average), channel_id=1, source_target_pairs={{0,513},{1,514},{2,515},{3,516},{4,517},{5,518},{6,519},{7,520},{8... | collective-permute-start | bytes 589832 | tf_op jit(solution)/shard_map/ppermute | solution.py:538
  71.1 0.9 copy-start
  72.0 0.9 copy-start.1
  72.9 28.5 %collective-permute-start.8 = (f32[3,8,2048]{2,1,0:T(8,128)S(1)}, f32[3,8,2048]{2,1,0:T(8,128)S(1)}, u32[]{:S(2)}, u32[]{:S(2)}) collective-permute-start(f32[3,8,2048]{2,1,0:T(8,128)S(1)} %shard_map.82), channel_id=1, source_target_pairs={{0,512},{1,513},{2,514},{3,515},{4,516},{5,517},{6,518},{7,519},{8... | collective-permute-start | bytes 589832 | tf_op jit(solution)/shard_map/ppermute | solution.py:555
